TPU v7x, 256 devices: a whole 4x4x8 slice. The times are simulated.
256 devices in a mesh: fsdp: 32 (over x_hi, z, core), tp: 8 (over x_lo, y).
Axes of the slice: x: 4 (x_hi: 2, x_lo: 2; x = x_hi * 2 + x_lo), y: 4, z: 8, core: 2. Of those that a mesh axis runs over, the one named last changes fastest.
Arguments:
- tokens: bfloat16 [4096, 3584], P('fsdp', 'tp'), may hold values from -6 to 6
- norm_gain: bfloat16 [3584], replicated, may hold values from 0.5 to 1.5
- gate_weight: bfloat16 [3584, 10240], P('fsdp', 'tp'), may hold values from -0.09375 to 0.09375
- up_weight: bfloat16 [3584, 10240], P('fsdp', 'tp'), may hold values from -0.09375 to 0.09375
- down_weight: bfloat16 [3584, 10240], P('fsdp', 'tp'), may hold values from -0.0625 to 0.0625
- probes: bfloat16 [2, 3584, 10240], P(None, 'fsdp', 'tp'), may hold values from -0.0625 to 0.0625
Outputs:
- layer_out: bfloat16 [4096, 3584], P('tp', 'fsdp')
- token_curv: float32 [4096], P('tp')
All inputs are finite; a program needn't handle non-finite values.
Results may differ from a plain program's by a relative error of at most 0.014.
Values may be sent and summed in bfloat16 or wider, within the bound.
A program may use at most 64 MiB of HBM per device.

v0:
```python
import jax
import jax.numpy as jnp
from jax import lax
from jax.sharding import PartitionSpec as P

D = 3584
PROBES = 2


epsilon = 1e-06


def in_order(blocks, dim):
    blocks = jnp.moveaxis(blocks, 0, dim)
    dims = blocks.shape
    return blocks.reshape(*dims[:dim], dims[dim] * dims[dim + 1], *dims[dim + 2 :])


def sent_to_all(array, axis):
    peers = lax.axis_size(axis)
    return lax.all_to_all(
        jnp.broadcast_to(array[None], (peers, *array.shape)), axis, 0, 0, tiled=True
    )


def gathered_copies(array, axis, dim):
    return in_order(sent_to_all(array, axis), dim)


def sent_together(arrays, axis, dim, along):
    ends, at = ([], 0)
    for a in arrays[:-1]:
        at += a.shape[along]
        ends.append(at)
    both = jnp.concatenate(arrays, axis=along)
    return tuple(jnp.split(lax.all_gather(both, axis, axis=dim, tiled=True), ends, axis=along))


def in_blocks(array, dim, peers):
    dims = array.shape
    blocks = array.reshape(*dims[:dim], peers, dims[dim] // peers, *dims[dim + 1 :])
    return jnp.moveaxis(blocks, dim, 0)


def summed_on_arrival(array, axis, dim):
    peers = lax.axis_size(axis)
    blocks = lax.all_to_all(in_blocks(array, dim, peers), axis, 0, 0, tiled=True)
    return jnp.sum(blocks.astype(jnp.float32), axis=0)


def of_everyone(array, axis):
    return sent_to_all(array, axis).sum(axis=0)


def on_device(tokens, norm_gain, gate_weight, up_weight, down_weight, probes):
    features = gathered_copies(tokens, "tp", 1)
    widened = features.astype(jnp.float32)
    inverse_rms = lax.rsqrt(jnp.mean(widened * widened, axis=1, keepdims=True) + epsilon)
    normed = (widened * inverse_rms * norm_gain.astype(jnp.float32)).astype(jnp.bfloat16)
    gate_full, up_full = sent_together((gate_weight, up_weight), "fsdp", 0, 1)
    gate_sum = jnp.dot(normed, gate_full, preferred_element_type=jnp.float32)
    up_sum = jnp.dot(normed, up_full, preferred_element_type=jnp.float32)
    hidden = (jax.nn.silu(gate_sum) * up_sum).astype(jnp.bfloat16)
    stacked = jnp.concatenate([down_weight[None], probes], axis=0)
    count = stacked.shape[0]
    col_width = stacked.shape[1]
    flat_weights = stacked.reshape(count * col_width, stacked.shape[2])
    partial_terms = lax.dot_general(
        lax.all_gather(hidden, "fsdp", axis=0, tiled=True),
        flat_weights,
        (((1,), (1,)), ((), ())),
        preferred_element_type=jnp.float32,
    )
    summed = summed_on_arrival(partial_terms.astype(jnp.bfloat16), "tp", 0)
    summed_parts = summed.reshape(summed.shape[0], count, col_width)
    primal = summed_parts[:, 0, :]
    tangents = summed_parts[:, 1:, :]
    squashed = jax.nn.sigmoid(primal)
    slope = squashed * (1.0 - squashed)
    tangent_sq = jnp.sum(tangents * tangents, axis=1)
    local_curv = jnp.sum(slope * tangent_sq, axis=1) / (PROBES * D)
    token_curv = of_everyone(local_curv, "fsdp")
    return (primal.astype(jnp.bfloat16), token_curv)


def solution(mesh):
    return jax.shard_map(
        on_device,
        mesh=mesh,
        in_specs=(
            P("fsdp", "tp"),
            P(),
            P("fsdp", "tp"),
            P("fsdp", "tp"),
            P("fsdp", "tp"),
            P(None, "fsdp", "tp"),
        ),
        out_specs=(P("tp", "fsdp"), P("tp")),
        check_vma=False,
    )
```

profile of v0, /device:TPU:1, one launch (start us, length us, event | category | flops | bytes accessed | tf_op | source)
XLA Modules:
  0.0 352.6 jit_solution(11822923586931489641)
XLA Ops:
  7.2 0.0 all-gather.3.cloned.1.call-start
  7.2 1.9 pad_maximum_fusion.1
  9.1 1.9 broadcast_in_dim.6
  11.1 5.9 %all-to-all-start = ((bf16[8,128,448]{1,2,0:T(8,128)(2,1)}), bf16[8,128,448]{1,2,0:T(8,128)(2,1)S(1)}, u32[]{:S(2)}, u32[]{:S(2)}) async-start(bf16[8,128,448]{1,2,0:T(8,128)(2,1)} %broadcast_in_dim.6), calls=%async_computation | async-start | bytes 1835008 | tf_op jit(solution)/shard_map/all_to_all | solution.py:21
  17.0 0.0 all-gather.5.cloned.1.call-start
  17.1 0.7 convert_element_type.38
  17.8 12.6 %all-to-all-done = bf16[8,128,448]{1,2,0:T(8,128)(2,1)S(1)} async-done(((bf16[8,128,448]{1,2,0:T(8,128)(2,1)}), bf16[8,128,448]{1,2,0:T(8,128)(2,1)S(1)}, u32[]{:S(2)}, u32[]{:S(2)}) %all-to-all-start) | async-done | bytes 917536 | tf_op jit(solution)/shard_map/all_to_all | solution.py:21
  30.3 0.5 multiply_reduce_fusion
  30.8 0.5 fusion.11
  31.4 130.5 %all-gather.3.cloned.1.call-done = bf16[3584,2560]{1,0:T(8,128)(2,1)} async-done(((bf16[112,2560]{1,0:T(8,128)(2,1)}), bf16[3584,2560]{1,0:T(8,128)(2,1)}) %all-gather.3.cloned.1.call-update) | async-done | bytes 18350096 | tf_op jit(solution)/shard_map/all_gather | solution.py:36
  161.8 5.1 %fusion.2 = f32[128,1280]{1,0:T(8,128)S(1)} fusion(bf16[128,3584]{0,1:T(8,128)(2,1)S(1)} %fusion.11, bf16[3584,2560]{1,0:T(8,128)(2,1)} %all-gather.3.cloned.1.call-done), kind=kOutput, calls=%fused_computation.2 | convolution fusion | flops 1174405120 | bytes 10747904 | tf_op jit(solution)/shard_map/dot_general | solution.py:61
  167.0 5.9 %fusion.7 = bf16[128,1280]{1,0:T(8,128)(2,1)} fusion(bf16[128,3584]{0,1:T(8,128)(2,1)S(1)} %fusion.11, bf16[3584,2560]{1,0:T(8,128)(2,1)} %all-gather.3.cloned.1.call-done, f32[128,1280]{1,0:T(8,128)S(1)} %fusion.2), kind=kOutput, calls=%fused_computation.8 | convolution fusion | flops 1175388160 | bytes 11075584 | tf_op jit(solution)/shard_map/dot_general | solution.py:62
  172.9 0.1 pad_maximum_fusion
  173.0 105.2 %all-gather.5.cloned.1.call-done = bf16[4096,1280]{1,0:T(8,128)(2,1)} async-done(((bf16[128,1280]{1,0:T(8,128)(2,1)}), bf16[4096,1280]{1,0:T(8,128)(2,1)}) %all-gather.5.cloned.1.call-update) | async-done | bytes 10485776 | tf_op jit(solution)/shard_map/all_gather | solution.py:69
  278.1 11.1 %convolution_convert_fusion = bf16[4096,336]{0,1:T(8,128)(2,1)S(1)} fusion(bf16[4096,1280]{1,0:T(8,128)(2,1)} %all-gather.5.cloned.1.call-done, bf16[336,1280]{1,0:T(8,128)(2,1)S(1)} %bitcast.28), kind=kOutput, calls=%fused_computation.5 | convolution fusion | flops 3524591616 | bytes 14098432 | tf_op jit(solution)/shard_map/dot_general | solution.py:68
  289.2 0.3 copy.16
  289.5 37.0 %all_to_all.16 = bf16[8,512,336]{1,2,0:T(8,128)(2,1)S(1)} all-to-all(bf16[8,512,336]{1,2,0:T(8,128)(2,1)S(1)} %bitcast.23), channel_id=1, replica_groups=mesh['fsdp'=32,'tp'=8] {'tp'}, dimensions={0} | all-to-all | bytes 5505024 | tf_op jit(solution)/shard_map/all_to_all | solution.py:47
  326.4 0.4 convert_reduce_fusion
  326.9 0.1 fusion.14
  327.0 0.7 broadcast_in_dim.8
  327.6 7.9 %all-to-all-start.2 = ((f32[32,1,512]{2,1,0:T(1,128)}), f32[32,1,512]{2,1,0:T(1,128)S(1)}, u32[]{:S(2)}, u32[]{:S(2)}) async-start(f32[32,1,512]{2,1,0:T(1,128)} %broadcast_in_dim.8), calls=%async_computation.2 | async-start | bytes 131072 | tf_op jit(solution)/shard_map/all_to_all | solution.py:21
  335.5 0.7 fusion.15
  336.2 8.9 %all-to-all-done.2 = f32[32,1,512]{2,1,0:T(1,128)S(1)} async-done(((f32[32,1,512]{2,1,0:T(1,128)}), f32[32,1,512]{2,1,0:T(1,128)S(1)}, u32[]{:S(2)}, u32[]{:S(2)}) %all-to-all-start.2) | async-done | bytes 65568 | tf_op jit(solution)/shard_map/all_to_all | solution.py:21
  345.1 0.6 reduce_sum.49
  (9 shorter events, 0.1 us)
Async XLA Ops:
  7.2 154.7 %all-gather.3.cloned.1.call-start = ((), (), s32[]{:S(2)}) async-start(), calls=%async_computation.3 | async-start | bytes 18923520 | tf_op jit(solution)/shard_map/all_gather | solution.py:36
  11.1 19.2 %all-to-all-start = ((bf16[8,128,448]{1,2,0:T(8,128)(2,1)}), bf16[8,128,448]{1,2,0:T(8,128)(2,1)S(1)}, u32[]{:S(2)}, u32[]{:S(2)}) async-start(bf16[8,128,448]{1,2,0:T(8,128)(2,1)} %broadcast_in_dim.6), calls=%async_computation | async-start | bytes 1835008 | tf_op jit(solution)/shard_map/all_to_all | solution.py:21
  17.0 261.1 %all-gather.5.cloned.1.call-start = ((), (), s32[]{:S(2)}) async-start(), calls=%async_computation.4 | async-start | bytes 10813440 | tf_op jit(solution)/shard_map/all_gather | solution.py:69
  167.0 5.9 %copy-start = (bf16[2,112,1280]{2,1,0:T(8,128)(2,1)S(1)}, bf16[2,112,1280]{2,1,0:T(8,128)(2,1)}, u32[]{:S(2)}) copy-start(bf16[2,112,1280]{2,1,0:T(8,128)(2,1)} %param.11) | copy-start | bytes 1720324
  167.0 5.9 %copy-start.1 = (bf16[112,1280]{1,0:T(8,128)(2,1)S(1)}, bf16[112,1280]{1,0:T(8,128)(2,1)}, u32[]{:S(2)}) copy-start(bf16[112,1280]{1,0:T(8,128)(2,1)} %param.10) | copy-start | bytes 860164
  327.6 17.5 %all-to-all-start.2 = ((f32[32,1,512]{2,1,0:T(1,128)}), f32[32,1,512]{2,1,0:T(1,128)S(1)}, u32[]{:S(2)}, u32[]{:S(2)}) async-start(f32[32,1,512]{2,1,0:T(1,128)} %broadcast_in_dim.8), calls=%async_computation.2 | async-start | bytes 131072 | tf_op jit(solution)/shard_map/all_to_all | solution.py:21
Sparse Core Ops, SparseCore 0:
  10.7 151.0 all-gather.2
  173.0 105.1 all-gather.4
where the time goes:
time: 353 us
  waiting for transfers between devices  257 us (73%)
  blocking collectives  37 us (10%)
  matrix products  22 us (6%)
  between operations  14.1 us (4%)
  starting transfers between devices  13.9 us (4%)
  other arithmetic  4.9 us (1%)
    all_gather x1, waiting for transfers between devices, sent_together(): lax.all_gather(both, axis, axis=dim, tiled=True)  130 us
    all_gather x1, waiting for transfers between devices, on_device(): lax.all_gather(hidden, 'fsdp', axis=0, tiled=True)  105 us
    all_to_all x1, blocking collectives, summed_on_arrival(): lax.all_to_all(in_blocks(array, dim, peers), axis, 0, 0, tiled=True)  37 us
    all_to_all x2, waiting for transfers between devices, sent_to_all(): lax.all_to_all(jnp.broadcast_to(array[None], (peers, *array.shape)), axis...  21.5 us
    all_to_all x2, starting transfers between devices, sent_to_all(): lax.all_to_all(jnp.broadcast_to(array[None], (peers, *array.shape)), axis...  13.8 us
    dot_general x1, matrix products, on_device(): lax.dot_general(lax.all_gather(hidden, 'fsdp', axis=0, tiled=True), flat_...  11.1 us
  transfers between devices with their start and end apart: 4, of which 4 were waited for; matrix products, arithmetic and copies ran while one was open for 1% of the time, Pallas kernels for 0%

commit v1 on v0

v1 whole, which is shorter than its diff:
```python
import jax
import jax.numpy as jnp
from jax import lax
from jax.experimental import pallas as pl
from jax.experimental.pallas import tpu as pltpu
from jax.sharding import PartitionSpec as P

MESH = pl.DeviceIdType.MESH
F32, BF16 = jnp.float32, jnp.bfloat16
D = 3584
PROBES = 2
EPS = 1e-06
KD = 112
FH = 640
TB = 128
DT = 448
XR = 224
NT = (((1,), (1,)), ((), ()))

SCRATCH = dict(
    xg=((8, 256, DT), BF16),
    xn=((8, 256, DT), BF16),
    w=((D, 2 * FH), BF16),
    acc=((256, 2 * FH), F32),
    h=((4096, FH), BF16),
    mx=((2, 3 * KD, FH), BF16),
    popp=((4, XR, 512), BF16),
    pr=((4, XR, 512), BF16),
    pl_=((4, XR, 512), BF16),
    ra=((4, XR, 256), BF16),
    rb=((4, XR, 256), BF16),
    rr=((4, XR, 512), BF16),
    rl=((4, XR, 512), BF16),
    s=((4, XR, 512), BF16),
    sf=((XR, 512), F32),
    ya=((XR, 256), BF16),
    yb=((XR, 256), BF16),
    yr=((XR, 512), BF16),
    yl=((XR, 512), BF16),
    q=((4, 4, KD, 512), BF16),
    qa=((2, KD, 512), BF16),
    qb=((2, KD, 512), BF16),
    qr=((4, KD, 512), BF16),
    ql=((4, KD, 512), BF16),
    tq=((4, KD, 512), BF16),
    tf=((KD, 512), F32),
    fa=((KD, 256), BF16),
    fb=((KD, 256), BF16),
    fr=((KD, 512), BF16),
    fl=((KD, 512), BF16),
    cvs=((3, 1, 512), F32),
    cvr=((10, 1, 512), F32),
)
SEMS = dict(
    tokx=(3,), toky=(2, 2, 2), w1=(2,), m1=(3,), wr=(2, 2, 4, 2), wd=(2, 8), hr=(2, 4, 2), hd=(8, 2),
    xa=(4, 2), xb=(4, 2, 2), qa=(2,), qb=(2, 2), ya=(2,), yb=(2, 2), fa=(2,), fb=(2, 2), cv=(10,),
)


class Refs:
    pass


def kernel(tok, gain, wg, wu, dn, pr, out, curv, *scratch):
    b, ss, rs = Refs(), Refs(), Refs()
    names = list(SCRATCH)
    for n, r in zip(names, scratch):
        setattr(b, n, r)
    rest = scratch[len(names):]
    for i, n in enumerate(SEMS):
        setattr(ss, n, rest[2 * i])
        setattr(rs, n, rest[2 * i + 1])
    loc = rest[2 * len(SEMS)]

    fi, ti = lax.axis_index("fsdp"), lax.axis_index("tp")
    X, z, c = fi // 16, lax.rem(fi // 2, 8), lax.rem(fi, 2)
    xl, y = ti // 4, lax.rem(ti, 4)
    x = X * 2 + xl

    def dev(x_=None, y_=None, z_=None, c_=None):
        x_ = x if x_ is None else x_
        y_ = y if y_ is None else y_
        z_ = z if z_ is None else z_
        c_ = c if c_ is None else c_
        return ((x_ // 2) * 16 + z_ * 2 + c_, lax.rem(x_, 2) * 4 + y_)

    xp, xm, xo = lax.rem(x + 1, 4), lax.rem(x + 3, 4), lax.rem(x + 2, 4)
    yp, ym = lax.rem(y + 1, 4), lax.rem(y + 3, 4)
    dxp, dxm, dxo = dev(x_=xp), dev(x_=xm), dev(x_=xo)
    dyp, dym = dev(y_=yp), dev(y_=ym)
    dz = (dev(z_=lax.rem(z + 1, 8)), dev(z_=lax.rem(z + 7, 8)))
    dc = dev(c_=1 - c)

    def copy(name, idx, src, dst, to):
        return pltpu.make_async_remote_copy(
            src_ref=src, dst_ref=dst, send_sem=getattr(ss, name).at[idx], recv_sem=getattr(rs, name).at[idx],
            device_id=to, device_id_type=MESH,
        )

    def send(name, idx, src, dst, to):
        copy(name, idx, src, dst, to).start()

    def got(name, idx, ref):
        copy(name, idx, ref, ref, dc).wait_recv()

    def sent(name, idx, ref):
        copy(name, idx, ref, ref, dc).wait_send()

    def cols(k):
        return pl.ds(pl.multiple_of(k * FH, 128), FH)

    def wrows(X_, z_, c_=None):
        c_ = c if c_ is None else c_
        return pl.ds(pl.multiple_of((X_ * 16 + z_ * 2 + c_) * KD, 16), KD)

    def wchunk(X_, z_, half):
        return b.w.at[wrows(X_, z_), pl.ds(half * FH, FH)]

    def hchunk(X_, z_):
        return b.h.at[pl.ds(pl.multiple_of((X_ * 16 + z_ * 2 + c) * TB, 128), TB), :]

    mine = [
        (tok, b.xg.at[ti, pl.ds(pl.multiple_of(X * TB, 128), TB), :]),
        (wg.at[:, cols(X)], wchunk(X, z, 0)),
        (wu.at[:, cols(X)], wchunk(X, z, 1)),
        (dn.at[:, cols(X)], b.mx.at[X, pl.ds(0, KD), :]),
        (pr.at[0, :, cols(X)], b.mx.at[X, pl.ds(KD, KD), :]),
        (pr.at[1, :, cols(X)], b.mx.at[X, pl.ds(2 * KD, KD), :]),
    ]
    own = [pltpu.make_async_copy(s_, d_, loc.at[i]) for i, (s_, d_) in enumerate(mine)]
    for o in own:
        o.start()

    barrier = pltpu.get_barrier_semaphore()
    zs = [lax.rem(z + r, 8) for r in range(8)]
    partners = [dxp, dxm, dxo, dyp, dym, dc] + [dev(z_=zs[r]) for r in range(1, 8)]
    for p in partners:
        pl.semaphore_signal(barrier, inc=1, device_id=p, device_id_type=MESH)
    pl.semaphore_wait(barrier, len(partners))

    for o in own:
        o.wait()

    def ring_start(sub, X_):
        for half in (0, 1):
            for d in (0, 1):
                send("wr", (d, sub, 0, half), wchunk(X_, z, half), wchunk(X_, z, half), dz[d])
        send("wd", (sub, 0), b.w.at[wrows(X_, z), :], b.w.at[wrows(X_, z), :], dc)

    ring_start(0, X)
    tx = b.xg.at[ti, pl.ds(pl.multiple_of(X * TB, 128), TB), :]
    for k, to in enumerate((dxp, dxm, dxo)):
        send("tokx", (k,), tok, tx, to)
    for half, src in enumerate((wg, wu)):
        send("w1", (half,), src.at[:, cols(1 - X)], wchunk(X, z, half), dxo)

    def m_send():
        for k, src in enumerate((dn, pr.at[0], pr.at[1])):
            send("m1", (k,), src.at[:, cols(1 - X)], b.mx.at[X, pl.ds(k * KD, KD), :], dxo)

    def zsrc(d, s_):
        return lax.rem(z + (8 - s_ if d == 0 else s_), 8)

    def ring_step(sub, X_, s_):
        for half in (0, 1):
            for d in (0, 1):
                if s_ == 4 and half != d:
                    continue
                ch = wchunk(X_, zsrc(d, s_), half)
                got("wr", (d, sub, s_ - 1, half), ch)
                if s_ < 3 or (s_ == 3 and half == d):
                    send("wr", (d, sub, s_, half), ch, ch, dz[d])
        for d in (0, 1):
            if s_ == 4 and d == 1:
                continue
            blk = b.w.at[wrows(X_, zsrc(d, s_)), :]
            send("wd", (sub, 8 - s_ if d == 0 else s_), blk, blk, dc)

    par = lax.rem(z, 2)

    def pair(i):
        f = 3 * i - 5 * (i // 2) - 2 * (i // 3)
        return lax.rem(z // 2 + f * (1 - par) + (4 - f) * par, 4)

    def other_core(sub, X_, s_):
        if s_ == 1:
            got("wd", (sub, 0), b.w.at[wrows(X_, z, 1 - c), :])
        for d in (0, 1):
            if s_ == 4 and d == 1:
                continue
            got("wd", (sub, 8 - s_ if d == 0 else s_), b.w.at[wrows(X_, zsrc(d, s_), 1 - c), :])

    def multiply(X_, s_):
        j = X_ * 4 + pair(s_ - 1)

        @pl.loop(0, 5)
        def _(n):
            cs = pl.ds(pl.multiple_of(n * 256, 256), 256)
            ks = pl.ds(pl.multiple_of(j * DT, 64), DT)
            b.acc[:, cs] += jnp.dot(b.xn[j], b.w[ks, cs], preferred_element_type=F32)

    def tokx_done():
        for k, sx in enumerate((xm, xp, xo)):
            got("tokx", (k,), b.xg.at[lax.rem(sx, 2) * 4 + y, pl.ds(pl.multiple_of((sx // 2) * TB, 128), TB), :])
        for k in (0, 1):
            blk = b.xg.at[k * 4 + y]
            send("toky", (0, k, 0), blk, blk, dyp)
            send("toky", (1, k, 0), blk, blk, dym)

    def toky_first():
        for d, sy, to in ((0, ym, dyp), (1, yp, dym)):
            for k in (0, 1):
                got("toky", (d, k, 0), b.xg.at[k * 4 + sy])
            blk = b.xg.at[d * 4 + sy]
            send("toky", (d, d, 1), blk, blk, to)

    def toky_last():
        for d in (0, 1):
            got("toky", (d, d, 1), b.xg.at[d * 4 + lax.rem(y + 2, 4)])

    def norm():
        @pl.loop(0, 8)
        def _(t):
            rows = pl.ds(pl.multiple_of(t * 32, 32), 32)
            total = jnp.zeros((32, 1), F32)
            for j in range(8):
                v = b.xg[j, rows, :].astype(F32)
                total += jnp.sum(v * v, axis=1, keepdims=True)
            inv = lax.rsqrt(total / D + EPS)
            for j in range(8):
                v = b.xg[j, rows, :].astype(F32)
                b.xn[j, rows, :] = (v * inv * gain[j : j + 1, :]).astype(BF16)

    b.acc[...] = jnp.zeros_like(b.acc)
    ring_step(0, X, 1)
    tokx_done()
    ring_step(0, X, 2)
    toky_first()
    ring_step(0, X, 3)
    for half in (0, 1):
        got("w1", (half,), wchunk(1 - X, z, half))
    ring_start(1, 1 - X)
    m_send()
    ring_step(0, X, 4)
    toky_last()
    norm()
    ring_step(1, 1 - X, 1)
    for s_ in (1, 2):
        other_core(0, X, s_)
        multiply(X, s_)
    ring_step(1, 1 - X, 2)
    for s_ in (3, 4):
        other_core(0, X, s_)
        multiply(X, s_)
    other_core(1, 1 - X, 1)
    multiply(1 - X, 1)
    ring_step(1, 1 - X, 3)
    other_core(1, 1 - X, 2)
    multiply(1 - X, 2)
    ring_step(1, 1 - X, 4)
    for s_ in (3, 4):
        other_core(1, 1 - X, s_)
        multiply(1 - X, s_)

    @pl.loop(0, 5)
    def _(n):
        cs = pl.ds(pl.multiple_of(n * 128, 128), 128)
        g = b.acc[:, cs]
        u = b.acc[:, pl.ds(pl.multiple_of(FH + n * 128, 128), 128)]
        hid = (g / (1.0 + jnp.exp(-g)) * u).astype(BF16)
        for k in (0, 1):
            b.h[pl.ds(pl.multiple_of((k * 16 + z * 2 + c) * TB, 128), TB), cs] = hid[k * TB : (k + 1) * TB]

    for k in (0, 1):
        for d in (0, 1):
            send("hr", (d, 0, k), hchunk(k, z), hchunk(k, z), dz[d])
        send("hd", (0, k), hchunk(k, z), hchunk(k, z), dc)
    for k in range(3):
        got("m1", (k,), b.mx.at[1 - X, pl.ds(k * KD, KD), :])

    def hother(k, z_):
        return b.h.at[pl.ds(pl.multiple_of((k * 16 + z_ * 2 + 1 - c) * TB, 128), TB), :]

    for k in (0, 1):
        got("hd", (0, k), hother(k, z))

    def h_step(s_):
        for k in (0, 1):
            for d in (0, 1):
                zz = lax.rem(z + (8 - s_ if d == 0 else s_), 8)
                r = 8 - s_ if d == 0 else s_
                ch = hchunk(k, zz)

                def take():
                    got("hr", (d, s_ - 1, k), ch)

                    @pl.when(s_ < (4 if k == d else 3))
                    def _():
                        send("hr", (d, s_, k), ch, ch, dz[d])

                    send("hd", (r, k), ch, ch, dc)

                if k == d:
                    take()
                else:
                    pl.when(s_ < 4)(take)
        for k in (0, 1):
            for d in (0, 1):
                zz = lax.rem(z + (8 - s_ if d == 0 else s_), 8)
                r = 8 - s_ if d == 0 else s_

                def take2():
                    got("hd", (r, k), hother(k, zz))

                if k == d:
                    take2()
                else:
                    pl.when(s_ < 4)(take2)

    def term(dx, k0, nk, m, lane, n):
        a = b.mx[dx // 2, k0 * KD : (k0 + nk) * KD, :]
        rows = pl.ds(pl.multiple_of(lax.rem(dx, 2) * 2048 + m * 512 + lane, 256), n)
        return lax.dot_general(a, b.h[rows, :], NT, preferred_element_type=F32)

    LO, HI = pl.ds(0, 256), pl.ds(256, 256)

    def rel_of(i):
        m = pair(i)
        return m, lax.rem(m - y + 4, 4)

    def part1(i):
        m, rel = rel_of(i)
        for k, lanes in enumerate((LO, HI)):
            b.popp[i, :, lanes] = term(xo, 1, 2, m, k * 256, 256).astype(BF16)
        send("xa", (i, 0), b.popp.at[i, :, LO], b.ra.at[i], dxp)
        send("xa", (i, 1), b.popp.at[i, :, HI], b.rb.at[i], dxm)
        b.pr[i, :, HI] = term(xp, 1, 2, m, 256, 256).astype(BF16)
        send("xb", (i, 0, 1), b.pr.at[i, :, HI], b.rr.at[i, :, HI], dxp)
        b.pl_[i, :, LO] = term(xm, 1, 2, m, 0, 256).astype(BF16)
        send("xb", (i, 1, 0), b.pl_.at[i, :, LO], b.rl.at[i, :, LO], dxm)
        for dx in range(4):
            a = b.mx[dx // 2, 0:KD, :]
            rows = pl.ds(pl.multiple_of((dx % 2) * 2048 + m * 512, 512), 512)
            b.q[i, dx] = lax.dot_general(a, b.h[rows, :], NT, preferred_element_type=F32).astype(BF16)
        lo, hi = b.q.at[i, pl.ds(0, 2)], b.q.at[i, pl.ds(2, 2)]

        @pl.when(rel == 2)
        def _():
            send("qa", (0,), lo, b.qa, dyp)
            send("qa", (1,), hi, b.qb, dym)

        @pl.when(rel == 1)
        def _():
            send("qb", (0, 1), hi, b.qr.at[pl.ds(2, 2)], dyp)

        @pl.when(rel == 3)
        def _():
            send("qb", (1, 0), lo, b.ql.at[pl.ds(0, 2)], dym)

    def part2(i):
        m, rel = rel_of(i)
        got("xa", (i, 0), b.ra.at[i])
        b.pr[i, :, LO] = (term(xp, 1, 2, m, 0, 256) + b.ra[i].astype(F32)).astype(BF16)
        send("xb", (i, 0, 0), b.pr.at[i, :, LO], b.rr.at[i, :, LO], dxp)
        got("xa", (i, 1), b.rb.at[i])
        b.pl_[i, :, HI] = (term(xm, 1, 2, m, 256, 256) + b.rb[i].astype(F32)).astype(BF16)
        send("xb", (i, 1, 1), b.pl_.at[i, :, HI], b.rl.at[i, :, HI], dxm)

        @pl.when(rel == 1)
        def _():
            got("qa", (0,), b.qa)
            for k in (0, 1):
                b.q[i, k] = (b.q[i, k].astype(F32) + b.qa[k].astype(F32)).astype(BF16)
            send("qb", (0, 0), b.q.at[i, pl.ds(0, 2)], b.qr.at[pl.ds(0, 2)], dyp)

        @pl.when(rel == 3)
        def _():
            got("qa", (1,), b.qb)
            for k in (0, 1):
                b.q[i, 2 + k] = (b.q[i, 2 + k].astype(F32) + b.qb[k].astype(F32)).astype(BF16)
            send("qb", (1, 1), b.q.at[i, pl.ds(2, 2)], b.ql.at[pl.ds(2, 2)], dym)

    def part3(i):
        m, rel = rel_of(i)
        for k, lanes in enumerate((LO, HI)):
            got("xb", (i, 0, k), b.rr.at[i, :, lanes])
            got("xb", (i, 1, k), b.rl.at[i, :, lanes])
            t = term(x, 1, 2, m, k * 256, 256) + b.rr[i, :, lanes].astype(F32) + b.rl[i, :, lanes].astype(F32)
            b.s[i, :, lanes] = t.astype(BF16)

            @pl.when(rel == 0)
            def _():
                b.sf[:, lanes] = t

        lo, hi = b.s.at[i, :, LO], b.s.at[i, :, HI]

        @pl.when(rel == 2)
        def _():
            send("ya", (0,), lo, b.ya, dyp)
            send("ya", (1,), hi, b.yb, dym)

        @pl.when(rel == 1)
        def _():
            send("yb", (0, 1), hi, b.yr.at[:, HI], dyp)

        @pl.when(rel == 3)
        def _():
            send("yb", (1, 0), lo, b.yl.at[:, LO], dym)

        @pl.when(rel == 0)
        def _():
            for k in (0, 1):
                got("qb", (0, k), b.qr.at[pl.ds(2 * k, 2)])
                got("qb", (1, k), b.ql.at[pl.ds(2 * k, 2)])

            @pl.loop(0, 4)
            def _(dx):
                t = b.q[i, dx].astype(F32) + b.qr[dx].astype(F32) + b.ql[dx].astype(F32)
                b.tq[dx] = t.astype(BF16)

                @pl.when(dx == x)
                def _():
                    b.tf[...] = t

            send("fa", (0,), b.tq.at[xo, :, LO], b.fa, dxp)
            send("fa", (1,), b.tq.at[xo, :, HI], b.fb, dxm)
            send("fb", (0, 1), b.tq.at[xp, :, HI], b.fr.at[:, HI], dxp)
            send("fb", (1, 0), b.tq.at[xm, :, LO], b.fl.at[:, LO], dxm)

    def part4(i):
        _, rel = rel_of(i)

        @pl.when(rel == 1)
        def _():
            got("ya", (0,), b.ya)
            b.s[i, :, LO] = (b.s[i, :, LO].astype(F32) + b.ya[...].astype(F32)).astype(BF16)
            send("yb", (0, 0), b.s.at[i, :, LO], b.yr.at[:, LO], dyp)

        @pl.when(rel == 3)
        def _():
            got("ya", (1,), b.yb)
            b.s[i, :, HI] = (b.s[i, :, HI].astype(F32) + b.yb[...].astype(F32)).astype(BF16)
            send("yb", (1, 1), b.s.at[i, :, HI], b.yl.at[:, HI], dym)

        @pl.when(rel == 0)
        def _():
            got("fa", (0,), b.fa)
            b.tq[xp, :, LO] = (b.tq[xp, :, LO].astype(F32) + b.fa[...].astype(F32)).astype(BF16)
            send("fb", (0, 0), b.tq.at[xp, :, LO], b.fr.at[:, LO], dxp)
            got("fa", (1,), b.fb)
            b.tq[xm, :, HI] = (b.tq[xm, :, HI].astype(F32) + b.fb[...].astype(F32)).astype(BF16)
            send("fb", (1, 1), b.tq.at[xm, :, HI], b.fl.at[:, HI], dxm)

    @pl.loop(0, 7)
    def _(t):
        @pl.when(t < 4)
        def _():
            h_step(t + 1)
            part1(t)

        @pl.when((t >= 1) & (t < 5))
        def _():
            part2(t - 1)

        @pl.when((t >= 2) & (t < 6))
        def _():
            part3(t - 2)

        @pl.when(t >= 3)
        def _():
            part4(t - 3)

    for lanes, k in ((LO, 0), (HI, 1)):
        got("yb", (0, k), b.yr.at[:, lanes])
        got("yb", (1, k), b.yl.at[:, lanes])
        got("fb", (0, k), b.fr.at[:, lanes])
        got("fb", (1, k), b.fl.at[:, lanes])
    for k, lanes in enumerate((LO, HI)):
        primal = b.tf[:, lanes] + b.fr[:, lanes].astype(F32) + b.fl[:, lanes].astype(F32)
        out[:, lanes] = primal.astype(BF16)
        tan = b.sf[:, lanes] + b.yr[:, lanes].astype(F32) + b.yl[:, lanes].astype(F32)
        sq = 1.0 / (1.0 + jnp.exp(-primal))
        slope = sq * (1.0 - sq)
        both = tan[:KD] * tan[:KD] + tan[KD:] * tan[KD:]
        b.cvs[0, :, lanes] = jnp.sum(slope * both, axis=0, keepdims=True)

    send("cv", (8,), b.cvs.at[0], b.cvr.at[8], dc)
    got("cv", (8,), b.cvr.at[8])
    b.cvs[1] = b.cvs[0] + b.cvr[8]
    send("cv", (9,), b.cvs.at[1], b.cvr.at[9], dxo)
    got("cv", (9,), b.cvr.at[9])
    b.cvs[2] = b.cvs[1] + b.cvr[9]
    for r in range(1, 8):
        send("cv", (r,), b.cvs.at[2], b.cvr.at[r], dev(z_=zs[r]))
    total = b.cvs[2]
    for r in range(1, 8):
        got("cv", (r,), b.cvr.at[r])
        total += b.cvr[r]
    curv[...] = total / (PROBES * D)

    for k in range(3):
        sent("tokx", (k,), tok)
        sent("m1", (k,), b.mx.at[0, pl.ds(0, KD), :])
    for d in (0, 1):
        for k in (0, 1):
            sent("toky", (d, k, 0), b.xg.at[0])
        sent("toky", (d, d, 1), b.xg.at[0])
        sent("w1", (d,), wchunk(X, z, 0))
        sent("qa", (d,), b.qa)
        sent("ya", (d,), b.ya)
        sent("fa", (d,), b.fa)
        for k in (0, 1):
            sent("qb", (d, k), b.qa)
            sent("yb", (d, k), b.ya)
            sent("fb", (d, k), b.fa)
    for sub in (0, 1):
        for r in range(8):
            sent("wd", (sub, r), b.w.at[wrows(X, z), :])
            sent("hd", (r, sub), hchunk(0, z))
        for s_ in range(4):
            for d in (0, 1):
                for half in (0, 1):
                    if s_ == 3 and half != d:
                        continue
                    sent("wr", (d, sub, s_, half), wchunk(X, z, 0))
                if s_ < 3 or sub == d:
                    sent("hr", (d, s_, sub), hchunk(0, z))
    for i in range(4):
        for d in (0, 1):
            sent("xa", (i, d), b.ra.at[0])
            for k in (0, 1):
                sent("xb", (i, d, k), b.ra.at[0])
    for r in range(1, 10):
        sent("cv", (r,), b.cvs.at[0])


def on_device(tokens, norm_gain, gate_weight, up_weight, down_weight, probes):
    vmem = pl.BlockSpec(memory_space=pltpu.VMEM)
    sems = []
    for shape in SEMS.values():
        sems += [pltpu.SemaphoreType.DMA(shape), pltpu.SemaphoreType.DMA(shape)]
    out, curv = pl.pallas_call(
        kernel,
        out_shape=(jax.ShapeDtypeStruct((KD, 512), BF16), jax.ShapeDtypeStruct((1, 512), F32)),
        in_specs=[vmem] * 6,
        out_specs=(vmem, vmem),
        scratch_shapes=[pltpu.VMEM(s, t) for s, t in SCRATCH.values()] + sems + [pltpu.SemaphoreType.DMA((6,))],
        compiler_params=pltpu.CompilerParams(
            collective_id=0, has_side_effects=True, vmem_limit_bytes=60 * 1024 * 1024
        ),
        name="mlp_curv",
    )(tokens, norm_gain.astype(F32).reshape(8, DT), gate_weight, up_weight, down_weight, probes)
    return out.T, curv.reshape(512)


def solution(mesh):
    return jax.shard_map(
        on_device,
        mesh=mesh,
        in_specs=(
            P("fsdp", "tp"),
            P(),
            P("fsdp", "tp"),
            P("fsdp", "tp"),
            P("fsdp", "tp"),
            P(None, "fsdp", "tp"),
        ),
        out_specs=(P("tp", "fsdp"), P("tp")),
        check_vma=False,
    )
```

time: 353 us -> 140 us (0.40)
  waiting for transfers between devices: 257 us -> 0 us
  Pallas kernels: 0 us -> 134 us
  blocking collectives: 37 us -> 0 us
  matrix products: 22 us -> 0 us
  starting transfers between devices: 13.9 us -> 0 us
  between operations: 14.1 us -> 0.65 us
  other arithmetic: 4.9 us -> 0 us
    all_gather x2 -> x0, waiting for transfers between devices: 236 us -> none  [the longest x1 130 us: sent_together(): lax.all_gather(both, axis, axis=dim, tiled=True)]
    pallas_call x0 -> x1, Pallas kernels: none -> 134 us  [on_device(): pl.pallas_call(kernel, out_shape=(jax.ShapeDtypeStruct((KD, 512), BF16),...]
    all_to_all x1 -> x0, blocking collectives: 37 us -> none  [summed_on_arrival(): lax.all_to_all(in_blocks(array, dim, peers), axis, 0, 0, tiled=True)]
    dot_general x3 -> x0, matrix products: 22 us -> none  [the longest x1 11.1 us: on_device(): lax.dot_general(lax.all_gather(hidden, 'fsdp', axis=0, tiled=True), flat_...]
    all_to_all x2 -> x0, waiting for transfers between devices: 21.5 us -> none  [sent_to_all(): lax.all_to_all(jnp.broadcast_to(array[None], (peers, *array.shape)), axis...]
    all_to_all x2 -> x0, starting transfers between devices: 13.8 us -> none  [sent_to_all(): lax.all_to_all(jnp.broadcast_to(array[None], (peers, *array.shape)), axis...]
    unnamed x4 -> x5, local copies, waits for them, and re-layouts: 0.01 us -> 3.77 us
  transfers between devices with their start and end apart: 4 -> 0, of which waited for: 4 -> 0; matrix products, arithmetic and copies ran while one was open for 1% -> 0% of each run, Pallas kernels for 0% -> 0%
where the time goes in v1:
time: 140 us; the launch traced here: 139 us
  Pallas kernels  134 us (96%)
  local copies, waits for them, and re-layouts  5.15 us (4%)
    pallas_call x1, Pallas kernels, on_device(): pl.pallas_call(kernel, out_shape=(jax.ShapeDtypeStruct((KD, 512), BF16),...  134 us
    unnamed x5, local copies, waits for them, and re-layouts  3.77 us

profile of v1, /device:TPU:1, one launch (start us, length us, event | category | flops | bytes accessed | tf_op | source)
XLA Modules:
  0.0 139.4 jit_solution(6360504562475518882)
XLA Ops:
  0.6 1.4 reshape.16.gain
  2.0 1.6 %copy.8.tok = bf16[128,448]{1,0:T(8,128)(2,1)} copy(bf16[128,448]{0,1:T(8,128)(2,1)} %param.6) | data formatting | bytes 229376 | tf_op args[0]
  3.6 133.6 %mlp_curv.1 = (bf16[112,512]{1,0:T(8,128)(2,1)}, f32[1,512]{1,0:T(1,128)}) custom-call(bf16[128,448]{1,0:T(8,128)(2,1)} %copy.8.tok, f32[8,448]{1,0:T(8,128)} %reshape.16.gain, bf16[112,1280]{1,0:T(8,128)(2,1)} %wg.1, bf16[112,1280]{1,0:T(8,128)(2,1)} %wu.1, bf16[112,1280]{1,0:T(8,128)(2,1)} %dn.1, bf16[2,112,1280]{2,1,0:T(8,128)(2,1)} %pr.1), custom_call_target="tpu_custom_call" | custom-call | tf_op jit(solution)/shard_map/mlp_curv/pallas_call | solution.py:542
  137.2 0.0 copy-start
  137.3 1.6 %copy.11 = bf16[512,112]{0,1:T(8,128)(2,1)} copy(bf16[512,112]{0,1:T(8,128)(2,1)} %bitcast.2) | data formatting | bytes 229376
  138.8 0.0 copy-done
  138.8 0.6 copy.12
Async XLA Ops:
  137.2 1.6 %copy-start = (f32[1,512]{1,0:T(1,128)S(1)}, f32[1,512]{1,0:T(1,128)}, u32[]{:S(2)}) copy-start(f32[1,512]{1,0:T(1,128)} %get-tuple-element.5) | copy-start | bytes 6148

commit v2 on v1

v2 whole, which is shorter than its diff:
```python
import jax
import jax.numpy as jnp
from jax import lax
from jax.experimental import pallas as pl
from jax.experimental.pallas import tpu as pltpu
from jax.sharding import PartitionSpec as P

MESH = pl.DeviceIdType.MESH
F32, BF16 = jnp.float32, jnp.bfloat16
D = 3584
PROBES = 2
EPS = 1e-06
KD = 112
FH = 640
TB = 128
DT = 448
XR = 224
NT = (((1,), (1,)), ((), ()))

SCRATCH = dict(
    xg=((8, 256, DT), BF16),
    xn=((8, 256, DT), BF16),
    g8=((8, DT), F32),
    w=((D, 2 * FH), BF16),
    acc=((256, 2 * FH), F32),
    h=((4096, FH), BF16),
    mx=((2, 3 * KD, FH), BF16),
    popp=((8, XR, 256), BF16),
    pr=((8, XR, 256), BF16),
    pl_=((8, XR, 256), BF16),
    dr=((8, XR, 128), F32),
    dl=((8, XR, 128), F32),
    ra=((8, XR, 128), BF16),
    rb=((8, XR, 128), BF16),
    rr=((8, XR, 256), BF16),
    rl=((8, XR, 256), BF16),
    s=((8, XR, 256), BF16),
    sf=((2, XR, 256), F32),
    ya=((2, XR, 128), BF16),
    yb=((2, XR, 128), BF16),
    yr=((2, XR, 256), BF16),
    yl=((2, XR, 256), BF16),
    q=((8, 4, KD, 256), BF16),
    qa=((2, 2, KD, 256), BF16),
    qb=((2, 2, KD, 256), BF16),
    qr=((2, 4, KD, 256), BF16),
    ql=((2, 4, KD, 256), BF16),
    tq=((2, 4, KD, 256), BF16),
    tf=((2, KD, 256), F32),
    fa=((2, KD, 128), BF16),
    fb=((2, KD, 128), BF16),
    fr=((2, KD, 256), BF16),
    fl=((2, KD, 256), BF16),
    cvs=((1, 512), F32),
    cvr=((32, 1, 512), F32),
)
SEMS = dict(
    tokx=(3,), toky=(2, 2, 2), w1=(2,), m1=(3,), wr=(2, 2, 4, 2), wd=(2, 8), hr=(2, 4, 2), hd=(8, 2),
    xa=(8, 2), xb=(8, 2, 2), qa=(2, 2), qb=(2, 2, 2), ya=(2, 2), yb=(2, 2, 2), fa=(2, 2), fb=(2, 2, 2), cv=(32,),
)


class Refs:
    pass


def kernel(tok_t, gain, wg, wu, dn, pr, out, curv, *scratch):
    b, ss, rs = Refs(), Refs(), Refs()
    names = list(SCRATCH)
    for n, r in zip(names, scratch):
        setattr(b, n, r)
    rest = scratch[len(names):]
    for i, n in enumerate(SEMS):
        setattr(ss, n, rest[2 * i])
        setattr(rs, n, rest[2 * i + 1])
    loc = rest[2 * len(SEMS)]

    fi, ti = lax.axis_index("fsdp"), lax.axis_index("tp")
    X, z, c = fi // 16, lax.rem(fi // 2, 8), lax.rem(fi, 2)
    xl, y = ti // 4, lax.rem(ti, 4)
    x = X * 2 + xl

    def dev(x_=None, y_=None, z_=None, c_=None):
        x_ = x if x_ is None else x_
        y_ = y if y_ is None else y_
        z_ = z if z_ is None else z_
        c_ = c if c_ is None else c_
        return ((x_ // 2) * 16 + z_ * 2 + c_, lax.rem(x_, 2) * 4 + y_)

    xp, xm, xo = lax.rem(x + 1, 4), lax.rem(x + 3, 4), lax.rem(x + 2, 4)
    yp, ym = lax.rem(y + 1, 4), lax.rem(y + 3, 4)
    dxp, dxm, dxo = dev(x_=xp), dev(x_=xm), dev(x_=xo)
    dyp, dym = dev(y_=yp), dev(y_=ym)
    dz = (dev(z_=lax.rem(z + 1, 8)), dev(z_=lax.rem(z + 7, 8)))
    dc = dev(c_=1 - c)

    def copy(name, idx, src, dst, to):
        return pltpu.make_async_remote_copy(
            src_ref=src, dst_ref=dst, send_sem=getattr(ss, name).at[idx], recv_sem=getattr(rs, name).at[idx],
            device_id=to, device_id_type=MESH,
        )

    def send(name, idx, src, dst, to):
        copy(name, idx, src, dst, to).start()

    def got(name, idx, ref):
        copy(name, idx, ref, ref, dc).wait_recv()

    def sent(name, idx, ref):
        copy(name, idx, ref, ref, dc).wait_send()

    def cols(k):
        return pl.ds(pl.multiple_of(k * FH, 128), FH)

    def wrows(X_, z_, c_=None):
        c_ = c if c_ is None else c_
        return pl.ds(pl.multiple_of((X_ * 16 + z_ * 2 + c_) * KD, 16), KD)

    def wchunk(X_, z_, half):
        return b.w.at[wrows(X_, z_), pl.ds(half * FH, FH)]

    def hchunk(X_, z_):
        return b.h.at[pl.ds(pl.multiple_of((X_ * 16 + z_ * 2 + c) * TB, 128), TB), :]

    mine = [
        (wg.at[:, cols(X)], wchunk(X, z, 0)),
        (wu.at[:, cols(X)], wchunk(X, z, 1)),
        (dn.at[:, cols(X)], b.mx.at[X, pl.ds(0, KD), :]),
        (pr.at[0, :, cols(X)], b.mx.at[X, pl.ds(KD, KD), :]),
        (pr.at[1, :, cols(X)], b.mx.at[X, pl.ds(2 * KD, KD), :]),
    ]
    own = [pltpu.make_async_copy(s_, d_, loc.at[i]) for i, (s_, d_) in enumerate(mine)]
    for o in own:
        o.start()

    tx = b.xg.at[ti, pl.ds(pl.multiple_of(X * TB, 128), TB), :]
    tx[...] = tok_t[...].T
    for j in range(8):
        at = j * DT
        while at < (j + 1) * DT:
            n = min(128 - at % 128, (j + 1) * DT - at)
            row, lane = at // 128, at % 128
            b.g8[j : j + 1, at - j * DT : at - j * DT + n] = gain[row : row + 1, lane : lane + n].astype(F32)
            at += n

    barrier = pltpu.get_barrier_semaphore()
    peers = [(lax.rem(fi + r, 32), ti) for r in range(1, 32)]
    partners = [dxp, dxm, dyp, dym] + peers
    for p in partners:
        pl.semaphore_signal(barrier, inc=1, device_id=p, device_id_type=MESH)
    pl.semaphore_wait(barrier, len(partners))

    for o in own:
        o.wait()

    def ring_start(sub, X_):
        for half in (0, 1):
            for d in (0, 1):
                send("wr", (d, sub, 0, half), wchunk(X_, z, half), wchunk(X_, z, half), dz[d])
        send("wd", (sub, 0), b.w.at[wrows(X_, z), :], b.w.at[wrows(X_, z), :], dc)

    ring_start(0, X)
    for k, to in enumerate((dxp, dxm, dxo)):
        send("tokx", (k,), tx, tx, to)
    for half, src in enumerate((wg, wu)):
        send("w1", (half,), src.at[:, cols(1 - X)], wchunk(X, z, half), dxo)

    def m_send():
        for k, src in enumerate((dn, pr.at[0], pr.at[1])):
            send("m1", (k,), src.at[:, cols(1 - X)], b.mx.at[X, pl.ds(k * KD, KD), :], dxo)

    def zsrc(d, s_):
        return lax.rem(z + (8 - s_ if d == 0 else s_), 8)

    def ring_step(sub, X_, s_):
        for half in (0, 1):
            for d in (0, 1):
                if s_ == 4 and half != d:
                    continue
                ch = wchunk(X_, zsrc(d, s_), half)
                got("wr", (d, sub, s_ - 1, half), ch)
                if s_ < 3 or (s_ == 3 and half == d):
                    send("wr", (d, sub, s_, half), ch, ch, dz[d])
        for d in (0, 1):
            if s_ == 4 and d == 1:
                continue
            blk = b.w.at[wrows(X_, zsrc(d, s_)), :]
            send("wd", (sub, 8 - s_ if d == 0 else s_), blk, blk, dc)

    par = lax.rem(z, 2)

    def pair(i):
        f = 3 * i - 5 * (i // 2) - 2 * (i // 3)
        return lax.rem(z // 2 + f * (1 - par) + (4 - f) * par, 4)

    def other_core(sub, X_, s_):
        if s_ == 1:
            got("wd", (sub, 0), b.w.at[wrows(X_, z, 1 - c), :])
        for d in (0, 1):
            if s_ == 4 and d == 1:
                continue
            got("wd", (sub, 8 - s_ if d == 0 else s_), b.w.at[wrows(X_, zsrc(d, s_), 1 - c), :])

    def multiply(X_, s_):
        j = X_ * 4 + pair(s_ - 1)

        @pl.loop(0, 5)
        def _(n):
            cs = pl.ds(pl.multiple_of(n * 256, 256), 256)
            ks = pl.ds(pl.multiple_of(j * DT, 64), DT)
            b.acc[:, cs] += jnp.dot(b.xn[j], b.w[ks, cs], preferred_element_type=F32)

    def tokx_done():
        for k, sx in enumerate((xm, xp, xo)):
            got("tokx", (k,), b.xg.at[lax.rem(sx, 2) * 4 + y, pl.ds(pl.multiple_of((sx // 2) * TB, 128), TB), :])
        for k in (0, 1):
            blk = b.xg.at[k * 4 + y]
            send("toky", (0, k, 0), blk, blk, dyp)
            send("toky", (1, k, 0), blk, blk, dym)

    def toky_first():
        for d, sy, to in ((0, ym, dyp), (1, yp, dym)):
            for k in (0, 1):
                got("toky", (d, k, 0), b.xg.at[k * 4 + sy])
            blk = b.xg.at[d * 4 + sy]
            send("toky", (d, d, 1), blk, blk, to)

    def toky_last():
        for d in (0, 1):
            got("toky", (d, d, 1), b.xg.at[d * 4 + lax.rem(y + 2, 4)])

    def norm():
        @pl.loop(0, 8)
        def _(t):
            rows = pl.ds(pl.multiple_of(t * 32, 32), 32)
            total = jnp.zeros((32, 1), F32)
            for j in range(8):
                v = b.xg[j, rows, :].astype(F32)
                total += jnp.sum(v * v, axis=1, keepdims=True)
            inv = lax.rsqrt(total / D + EPS)
            for j in range(8):
                v = b.xg[j, rows, :].astype(F32)
                b.xn[j, rows, :] = (v * inv * b.g8[j : j + 1, :]).astype(BF16)

    b.acc[...] = jnp.zeros_like(b.acc)
    ring_step(0, X, 1)
    tokx_done()
    ring_step(0, X, 2)
    ring_step(0, X, 3)
    for half in (0, 1):
        got("w1", (half,), wchunk(1 - X, z, half))
    ring_start(1, 1 - X)
    toky_first()
    m_send()
    ring_step(0, X, 4)
    toky_last()
    norm()
    for s_ in (1, 2):
        other_core(0, X, s_)
        multiply(X, s_)
    ring_step(1, 1 - X, 1)
    for s_ in (3, 4):
        other_core(0, X, s_)
        multiply(X, s_)
    ring_step(1, 1 - X, 2)
    other_core(1, 1 - X, 1)
    multiply(1 - X, 1)
    ring_step(1, 1 - X, 3)
    for s_ in (2, 3):
        other_core(1, 1 - X, s_)
        multiply(1 - X, s_)
    ring_step(1, 1 - X, 4)
    other_core(1, 1 - X, 4)
    multiply(1 - X, 4)

    @pl.loop(0, 5)
    def _(n):
        cs = pl.ds(pl.multiple_of(n * 128, 128), 128)
        g = b.acc[:, cs]
        u = b.acc[:, pl.ds(pl.multiple_of(FH + n * 128, 128), 128)]
        hid = (g / (1.0 + jnp.exp(-g)) * u).astype(BF16)
        for k in (0, 1):
            b.h[pl.ds(pl.multiple_of((k * 16 + z * 2 + c) * TB, 128), TB), cs] = hid[k * TB : (k + 1) * TB]

    for k in (0, 1):
        for d in (0, 1):
            send("hr", (d, 0, k), hchunk(k, z), hchunk(k, z), dz[d])
        send("hd", (0, k), hchunk(k, z), hchunk(k, z), dc)
    for k in range(3):
        got("m1", (k,), b.mx.at[1 - X, pl.ds(k * KD, KD), :])

    def hother(k, z_):
        return b.h.at[pl.ds(pl.multiple_of((k * 16 + z_ * 2 + 1 - c) * TB, 128), TB), :]

    def h_take(s_):
        for k in (0, 1):
            for d in (0, 1):
                zz = lax.rem(z + (8 - s_ if d == 0 else s_), 8)
                r = 8 - s_ if d == 0 else s_
                ch = hchunk(k, zz)

                def take():
                    got("hr", (d, s_ - 1, k), ch)

                    @pl.when(s_ < (4 if k == d else 3))
                    def _():
                        send("hr", (d, s_, k), ch, ch, dz[d])

                    send("hd", (r, k), ch, ch, dc)

                if k == d:
                    take()
                else:
                    pl.when(s_ < 4)(take)

    def level(i):
        k = (i + 1) // 2
        r = lax.rem(i, 2) * (8 - 2 * k) + k
        return lax.rem(r, 8), lax.rem(z + r, 8)

    def term(dx, k0, nk, zz):
        a = b.mx[dx // 2, k0 * KD : (k0 + nk) * KD, :]
        rows = pl.ds(pl.multiple_of(lax.rem(dx, 2) * 2048 + zz * 256, 256), 256)
        return lax.dot_general(a, b.h[rows, :], NT, preferred_element_type=F32)

    LO, HI = pl.ds(0, 128), pl.ds(128, 128)
    HALVES = ((0, LO), (1, HI))

    def place(i):
        _, zz = level(i)
        return zz, lax.rem(zz, 2), lax.rem(zz // 2 - y + 4, 4)

    def plus(u, v):
        return (u.astype(F32) + v.astype(F32)).astype(BF16)

    def part1(i):
        zz, e, rel = place(i)
        r, _ = level(i)
        for k in (0, 1):
            got("hd", (r, k), hother(k, zz))
        b.popp[i] = term(xo, 1, 2, zz).astype(BF16)
        send("xa", (i, 0), b.popp.at[i, :, LO], b.ra.at[i], dxp)
        send("xa", (i, 1), b.popp.at[i, :, HI], b.rb.at[i], dxm)
        t = term(xp, 1, 2, zz)
        b.pr[i, :, HI] = t[:, 128:].astype(BF16)
        send("xb", (i, 0, 1), b.pr.at[i, :, HI], b.rr.at[i, :, HI], dxp)
        b.dr[i] = t[:, :128]
        t = term(xm, 1, 2, zz)
        b.pl_[i, :, LO] = t[:, :128].astype(BF16)
        send("xb", (i, 1, 0), b.pl_.at[i, :, LO], b.rl.at[i, :, LO], dxm)
        b.dl[i] = t[:, 128:]
        for dx in range(4):
            b.q[i, dx] = term(dx, 0, 1, zz).astype(BF16)
        lo, hi = b.q.at[i, pl.ds(0, 2)], b.q.at[i, pl.ds(2, 2)]

        @pl.when(rel == 2)
        def _():
            send("qa", (e, 0), lo, b.qa.at[e], dyp)
            send("qa", (e, 1), hi, b.qb.at[e], dym)

        @pl.when(rel == 1)
        def _():
            send("qb", (e, 0, 1), hi, b.qr.at[e, pl.ds(2, 2)], dyp)

        @pl.when(rel == 3)
        def _():
            send("qb", (e, 1, 0), lo, b.ql.at[e, pl.ds(0, 2)], dym)

    def part2(i):
        zz, e, rel = place(i)
        got("xa", (i, 0), b.ra.at[i])
        b.pr[i, :, LO] = (b.dr[i] + b.ra[i].astype(F32)).astype(BF16)
        send("xb", (i, 0, 0), b.pr.at[i, :, LO], b.rr.at[i, :, LO], dxp)
        got("xa", (i, 1), b.rb.at[i])
        b.pl_[i, :, HI] = (b.dl[i] + b.rb[i].astype(F32)).astype(BF16)
        send("xb", (i, 1, 1), b.pl_.at[i, :, HI], b.rl.at[i, :, HI], dxm)

        @pl.when(rel == 1)
        def _():
            got("qa", (e, 0), b.qa.at[e])
            for k in (0, 1):
                b.q[i, k] = plus(b.q[i, k], b.qa[e, k])
            send("qb", (e, 0, 0), b.q.at[i, pl.ds(0, 2)], b.qr.at[e, pl.ds(0, 2)], dyp)

        @pl.when(rel == 3)
        def _():
            got("qa", (e, 1), b.qb.at[e])
            for k in (0, 1):
                b.q[i, 2 + k] = plus(b.q[i, 2 + k], b.qb[e, k])
            send("qb", (e, 1, 1), b.q.at[i, pl.ds(2, 2)], b.ql.at[e, pl.ds(2, 2)], dym)

    def part3(i):
        zz, e, rel = place(i)
        for k, lanes in HALVES:
            got("xb", (i, 0, k), b.rr.at[i, :, lanes])
            got("xb", (i, 1, k), b.rl.at[i, :, lanes])
        t = term(x, 1, 2, zz) + b.rr[i].astype(F32) + b.rl[i].astype(F32)
        b.s[i] = t.astype(BF16)
        lo, hi = b.s.at[i, :, LO], b.s.at[i, :, HI]

        @pl.when(rel == 2)
        def _():
            send("ya", (e, 0), lo, b.ya.at[e], dyp)
            send("ya", (e, 1), hi, b.yb.at[e], dym)

        @pl.when(rel == 1)
        def _():
            send("yb", (e, 0, 1), hi, b.yr.at[e, :, HI], dyp)

        @pl.when(rel == 3)
        def _():
            send("yb", (e, 1, 0), lo, b.yl.at[e, :, LO], dym)

        @pl.when(rel == 0)
        def _():
            b.sf[e] = t
            for k in (0, 1):
                got("qb", (e, 0, k), b.qr.at[e, pl.ds(2 * k, 2)])
                got("qb", (e, 1, k), b.ql.at[e, pl.ds(2 * k, 2)])

            @pl.loop(0, 4)
            def _(dx):
                u = b.q[i, dx].astype(F32) + b.qr[e, dx].astype(F32) + b.ql[e, dx].astype(F32)
                b.tq[e, dx] = u.astype(BF16)

                @pl.when(dx == x)
                def _():
                    b.tf[e] = u

            send("fa", (e, 0), b.tq.at[e, xo, :, LO], b.fa.at[e], dxp)
            send("fa", (e, 1), b.tq.at[e, xo, :, HI], b.fb.at[e], dxm)
            send("fb", (e, 0, 1), b.tq.at[e, xp, :, HI], b.fr.at[e, :, HI], dxp)
            send("fb", (e, 1, 0), b.tq.at[e, xm, :, LO], b.fl.at[e, :, LO], dxm)

    def part4(i):
        _, e, rel = place(i)

        @pl.when(rel == 1)
        def _():
            got("ya", (e, 0), b.ya.at[e])
            b.s[i, :, LO] = plus(b.s[i, :, LO], b.ya[e])
            send("yb", (e, 0, 0), b.s.at[i, :, LO], b.yr.at[e, :, LO], dyp)

        @pl.when(rel == 3)
        def _():
            got("ya", (e, 1), b.yb.at[e])
            b.s[i, :, HI] = plus(b.s[i, :, HI], b.yb[e])
            send("yb", (e, 1, 1), b.s.at[i, :, HI], b.yl.at[e, :, HI], dym)

        @pl.when(rel == 0)
        def _():
            got("fa", (e, 0), b.fa.at[e])
            b.tq[e, xp, :, LO] = plus(b.tq[e, xp, :, LO], b.fa[e])
            send("fb", (e, 0, 0), b.tq.at[e, xp, :, LO], b.fr.at[e, :, LO], dxp)
            got("fa", (e, 1), b.fb.at[e])
            b.tq[e, xm, :, HI] = plus(b.tq[e, xm, :, HI], b.fb[e])
            send("fb", (e, 1, 1), b.tq.at[e, xm, :, HI], b.fl.at[e, :, HI], dxm)

    LAG2, LAG3, LAG4 = 1, 2, 3

    @pl.loop(0, 8 + LAG4)
    def _(t):
        @pl.when((lax.rem(t, 2) == 1) & (t < 8))
        def _():
            h_take((t + 1) // 2)

        @pl.when(t < 8)
        def _():
            part1(t)

        @pl.when((t >= LAG2) & (t < 8 + LAG2))
        def _():
            part2(t - LAG2)

        @pl.when((t >= LAG3) & (t < 8 + LAG3))
        def _():
            part3(t - LAG3)

        @pl.when(t >= LAG4)
        def _():
            part4(t - LAG4)

    for e in (0, 1):
        for k, lanes in HALVES:
            got("yb", (e, 0, k), b.yr.at[e, :, lanes])
            got("yb", (e, 1, k), b.yl.at[e, :, lanes])
            got("fb", (e, 0, k), b.fr.at[e, :, lanes])
            got("fb", (e, 1, k), b.fl.at[e, :, lanes])
        primal = b.tf[e] + b.fr[e].astype(F32) + b.fl[e].astype(F32)
        out[:, e * 256 : (e + 1) * 256] = primal.astype(BF16)
        tan = b.sf[e] + b.yr[e].astype(F32) + b.yl[e].astype(F32)
        sq = 1.0 / (1.0 + jnp.exp(-primal))
        slope = sq * (1.0 - sq)
        both = tan[:KD] * tan[:KD] + tan[KD:] * tan[KD:]
        b.cvs[:, e * 256 : (e + 1) * 256] = jnp.sum(slope * both, axis=0, keepdims=True)

    for r in range(1, 32):
        send("cv", (r,), b.cvs, b.cvr.at[r], peers[r - 1])
    total = b.cvs[...]
    for r in range(1, 32):
        got("cv", (r,), b.cvr.at[r])
        total += b.cvr[r]
    curv[...] = total / (PROBES * D)

    for k in range(3):
        sent("tokx", (k,), tx)
        sent("m1", (k,), b.mx.at[0, pl.ds(0, KD), :])
    for d in (0, 1):
        for k in (0, 1):
            sent("toky", (d, k, 0), b.xg.at[0])
        sent("toky", (d, d, 1), b.xg.at[0])
        sent("w1", (d,), wchunk(X, z, 0))
        for e in (0, 1):
            sent("qa", (e, d), b.qa.at[0])
            sent("ya", (e, d), b.ya.at[0])
            sent("fa", (e, d), b.fa.at[0])
            for k in (0, 1):
                sent("qb", (e, d, k), b.qa.at[0])
                sent("yb", (e, d, k), b.ya.at[0])
                sent("fb", (e, d, k), b.fa.at[0])
    for sub in (0, 1):
        for r in range(8):
            sent("wd", (sub, r), b.w.at[wrows(X, z), :])
            sent("hd", (r, sub), hchunk(0, z))
        for s_ in range(4):
            for d in (0, 1):
                for half in (0, 1):
                    if s_ == 3 and half != d:
                        continue
                    sent("wr", (d, sub, s_, half), wchunk(X, z, 0))
                if s_ < 3 or sub == d:
                    sent("hr", (d, s_, sub), hchunk(0, z))
    for i in range(8):
        for d in (0, 1):
            sent("xa", (i, d), b.ra.at[0])
            for k in (0, 1):
                sent("xb", (i, d, k), b.ra.at[0])
    for r in range(1, 32):
        sent("cv", (r,), b.cvs)


def on_device(tokens, norm_gain, gate_weight, up_weight, down_weight, probes):
    vmem = pl.BlockSpec(memory_space=pltpu.VMEM)
    sems = []
    for shape in SEMS.values():
        sems += [pltpu.SemaphoreType.DMA(shape), pltpu.SemaphoreType.DMA(shape)]
    out, curv = pl.pallas_call(
        kernel,
        out_shape=(jax.ShapeDtypeStruct((KD, 512), BF16), jax.ShapeDtypeStruct((1, 512), F32)),
        in_specs=[vmem] * 6,
        out_specs=(vmem, vmem),
        scratch_shapes=[pltpu.VMEM(s, t) for s, t in SCRATCH.values()] + sems + [pltpu.SemaphoreType.DMA((5,))],
        compiler_params=pltpu.CompilerParams(
            collective_id=0, has_side_effects=True, vmem_limit_bytes=60 * 1024 * 1024
        ),
        name="mlp_curv",
    )(tokens.T, norm_gain.reshape(28, 128), gate_weight, up_weight, down_weight, probes)
    return out.T, curv.reshape(512)


def solution(mesh):
    return jax.shard_map(
        on_device,
        mesh=mesh,
        in_specs=(
            P("fsdp", "tp"),
            P(),
            P("fsdp", "tp"),
            P("fsdp", "tp"),
            P("fsdp", "tp"),
            P(None, "fsdp", "tp"),
        ),
        out_specs=(P("tp", "fsdp"), P("tp")),
        check_vma=False,
    )
```

time: 140 us -> 140 us (level)
  local copies, waits for them, and re-layouts: 5.15 us -> 2.14 us
  Pallas kernels: 134 us -> 137 us
    pallas_call x1, Pallas kernels: 134 us -> 137 us  [on_device(): pl.pallas_call(kernel, out_shape=(jax.ShapeDtypeStruct((KD, 512), BF16),...]
    unnamed x5 -> x4, local copies, waits for them, and re-layouts: 3.77 us -> 2.14 us
where the time goes in v2:
time: 140 us
  Pallas kernels  137 us (98%)
  local copies, waits for them, and re-layouts  2.14 us (2%)
    pallas_call x1, Pallas kernels, on_device(): pl.pallas_call(kernel, out_shape=(jax.ShapeDtypeStruct((KD, 512), BF16),...  137 us

profile of v2, /device:TPU:1, one launch (start us, length us, event | category | flops | bytes accessed | tf_op | source)
XLA Modules:
  0.0 139.6 jit_solution(1054551538055465278)
XLA Ops:
  0.6 136.8 %mlp_curv.1 = (bf16[112,512]{1,0:T(8,128)(2,1)}, f32[1,512]{1,0:T(1,128)}) custom-call(bf16[448,128]{1,0:T(8,128)(2,1)} %bitcast.4, bf16[28,128]{1,0:T(8,128)(2,1)} %bitcast.6, bf16[112,1280]{1,0:T(8,128)(2,1)} %wg.1, bf16[112,1280]{1,0:T(8,128)(2,1)} %wu.1, bf16[112,1280]{1,0:T(8,128)(2,1)} %dn.1, bf16[2,112,1280]{2,1,0:T(8,128)(2,1)} %pr.1), custom_call_target="tpu_custom_call" | custom-call | tf_op jit(solution)/shard_map/mlp_curv/pallas_call | solution.py:547
  137.4 0.0 copy-start
  137.4 1.6 %copy.10 = bf16[512,112]{0,1:T(8,128)(2,1)} copy(bf16[512,112]{0,1:T(8,128)(2,1)} %bitcast.5) | data formatting | bytes 229376
  139.0 0.0 copy-done
  139.0 0.6 copy.11
Async XLA Ops:
  137.4 1.6 %copy-start = (f32[1,512]{1,0:T(1,128)S(1)}, f32[1,512]{1,0:T(1,128)}, u32[]{:S(2)}) copy-start(f32[1,512]{1,0:T(1,128)} %get-tuple-element.5) | copy-start | bytes 6148

commit v3 on v2

v3 whole, which is shorter than its diff:
```python
import jax
import jax.numpy as jnp
from jax import lax
from jax.experimental import pallas as pl
from jax.experimental.pallas import tpu as pltpu
from jax.sharding import PartitionSpec as P

MESH = pl.DeviceIdType.MESH
F32, BF16 = jnp.float32, jnp.bfloat16
D = 3584
PROBES = 2
EPS = 1e-06
KD = 112
FH = 640
TB = 128
DT = 448
NY, NX = 2 * KD, KD

SCRATCH = dict(
    xg=((8, 256, DT), BF16),
    xn=((8, 256, DT), BF16),
    g8=((8, DT), F32),
    w=((D, 2 * FH), BF16),
    acc=((256, 2 * FH), F32),
    hs=((2, FH, TB), BF16),
    h=((32, FH, TB), BF16),
    mx=((2, 3 * KD, 2 * FH), BF16),
    px=((8, 2, NX, TB), BF16),
    rx=((8, 2, NX, TB), BF16),
    sx=((8, 2, NX, TB), F32),
    s=((8, 2, NX, TB), BF16),
    ya=((2, NX, TB), BF16),
    yb=((2, NX, TB), BF16),
    yr=((2, 2, NX, TB), BF16),
    yl=((2, 2, NX, TB), BF16),
    us=((2, 2, NX, TB), BF16),
    fs=((2, 2, NX, TB), BF16),
    q=((8, 2, 2, NY, TB), BF16),
    qa=((2, 2, NY, TB), BF16),
    qb=((2, 2, NY, TB), BF16),
    qr=((2, 2, 2, NY, TB), BF16),
    ql=((2, 2, 2, NY, TB), BF16),
    tq=((2, 2, 2, NY, TB), BF16),
    fq=((4, 2, NY, TB), BF16),
    ov=((KD, 512), BF16),
    cvo=((1, 512), F32),
    cvs=((1, 512), F32),
    cvr=((32, 1, 512), F32),
)
SEMS = dict(
    tokx=(3,), toky=(2, 2, 2), w1=(1,), m1=(1,), wr=(2, 2, 4, 2), wd=(2, 8), hx=(2,), hr=(2, 4, 2), hd=(8, 2),
    px=(8,), qa=(2, 2), qr=(2, 2), ya=(2, 2), yr=(2, 2), fq=(2,), fs=(2,), cv=(1,),
)


class Refs:
    pass


def kernel(tok_t, gain, wg, wu, dn, pr, out, curv, *scratch):
    b, ss, rs = Refs(), Refs(), Refs()
    names = list(SCRATCH)
    for n, r in zip(names, scratch):
        setattr(b, n, r)
    rest = scratch[len(names):]
    for i, n in enumerate(SEMS):
        setattr(ss, n, rest[2 * i])
        setattr(rs, n, rest[2 * i + 1])
    loc = rest[2 * len(SEMS)]

    fi, ti = lax.axis_index("fsdp"), lax.axis_index("tp")
    X, z, c = fi // 16, lax.rem(fi // 2, 8), lax.rem(fi, 2)
    xl, y = ti // 4, lax.rem(ti, 4)
    x = X * 2 + xl

    def dev(x_=None, y_=None, z_=None, c_=None):
        x_ = x if x_ is None else x_
        y_ = y if y_ is None else y_
        z_ = z if z_ is None else z_
        c_ = c if c_ is None else c_
        return ((x_ // 2) * 16 + z_ * 2 + c_, lax.rem(x_, 2) * 4 + y_)

    xp, xm, xo = lax.rem(x + 1, 4), lax.rem(x + 3, 4), lax.rem(x + 2, 4)
    yp, ym = lax.rem(y + 1, 4), lax.rem(y + 3, 4)
    dxp, dxm, dxo = dev(x_=xp), dev(x_=xm), dev(x_=xo)
    dyp, dym = dev(y_=yp), dev(y_=ym)
    dz = (dev(z_=lax.rem(z + 1, 8)), dev(z_=lax.rem(z + 7, 8)))
    dc = dev(c_=1 - c)

    def copy(name, idx, src, dst, to):
        out_sem = getattr(ss, name).at[idx[0] if name == "tokx" else 0]
        return pltpu.make_async_remote_copy(
            src_ref=src, dst_ref=dst, send_sem=out_sem, recv_sem=getattr(rs, name).at[idx],
            device_id=to, device_id_type=MESH,
        )

    def send(name, idx, src, dst, to):
        copy(name, idx, src, dst, to).start()

    def got(name, idx, ref):
        copy(name, idx, ref, ref, dc).wait_recv()

    def sent(name, ref, idx=0):
        copy(name, (idx,) + (0,) * (len(SEMS[name]) - 1), ref, ref, dc).wait_send()

    def cols(k):
        return pl.ds(pl.multiple_of(k * FH, 128), FH)

    def wrows(X_, z_, c_=None):
        c_ = c if c_ is None else c_
        return pl.ds(pl.multiple_of((X_ * 16 + z_ * 2 + c_) * KD, 16), KD)

    def wchunk(X_, z_, half):
        return b.w.at[wrows(X_, z_), pl.ds(half * FH, FH)]

    def hchunk(X_, z_):
        return b.h.at[c * 16 + X_ * 8 + z_]

    mine = [
        (wg.at[:, cols(X)], wchunk(X, z, 0)),
        (wu.at[:, cols(X)], wchunk(X, z, 1)),
        (dn, b.mx.at[X, pl.ds(0, KD), :]),
        (pr.at[0], b.mx.at[X, pl.ds(KD, KD), :]),
        (pr.at[1], b.mx.at[X, pl.ds(2 * KD, KD), :]),
    ]
    own = [pltpu.make_async_copy(s_, d_, loc.at[i]) for i, (s_, d_) in enumerate(mine)]
    for o in own:
        o.start()

    tx = b.xg.at[ti, pl.ds(pl.multiple_of(X * TB, 128), TB), :]
    tx[...] = tok_t[...].T
    for j in range(8):
        at = j * DT
        while at < (j + 1) * DT:
            n = min(128 - at % 128, (j + 1) * DT - at)
            row, lane = at // 128, at % 128
            b.g8[j : j + 1, at - j * DT : at - j * DT + n] = gain[row : row + 1, lane : lane + n].astype(F32)
            at += n

    barrier = pltpu.get_barrier_semaphore()
    peers = [(lax.rem(fi + r, 32), ti) for r in range(1, 32)]
    partners = [dxp, dxm, dyp, dym] + peers
    for p in partners:
        pl.semaphore_signal(barrier, inc=1, device_id=p, device_id_type=MESH)
    pl.semaphore_wait(barrier, len(partners))

    for o in own:
        o.wait()

    def ring_start(sub, X_):
        for half in (0, 1):
            for d in (0, 1):
                send("wr", (d, sub, 0, half), wchunk(X_, z, half), wchunk(X_, z, half), dz[d])
        send("wd", (sub, 0), b.w.at[wrows(X_, z), :], b.w.at[wrows(X_, z), :], dc)

    ring_start(0, X)
    for k, to in enumerate((dxp, dxm, dxo)):
        send("tokx", (k,), tx, tx, to)
    for half, src in enumerate((wg, wu)):
        send("w1", (0,), src.at[:, cols(1 - X)], wchunk(X, z, half), dxo)

    def m_send():
        for k, src in enumerate((dn, pr.at[0], pr.at[1])):
            send("m1", (0,), src, b.mx.at[X, pl.ds(k * KD, KD), :], dxo)

    def zsrc(d, s_):
        return lax.rem(z + (8 - s_ if d == 0 else s_), 8)

    def ring_half(sub, X_, s_, half):
        for d in (0, 1):
            if s_ == 4 and half != d:
                continue
            ch = wchunk(X_, zsrc(d, s_), half)
            got("wr", (d, sub, s_ - 1, half), ch)
            if s_ < 3 or (s_ == 3 and half == d):
                send("wr", (d, sub, s_, half), ch, ch, dz[d])
        if half == 1:
            for d in (0, 1):
                if s_ == 4 and d == 1:
                    continue
                blk = b.w.at[wrows(X_, zsrc(d, s_)), :]
                send("wd", (sub, 8 - s_ if d == 0 else s_), blk, blk, dc)

    par = lax.rem(z, 2)

    def pair(i):
        f = 3 * i - 5 * (i // 2) - 2 * (i // 3)
        return lax.rem(z // 2 + f * (1 - par) + (4 - f) * par, 4)

    def other_core(sub, X_, s_):
        if s_ == 1:
            got("wd", (sub, 0), b.w.at[wrows(X_, z, 1 - c), :])
        for d in (0, 1):
            if s_ == 4 and d == 1:
                continue
            got("wd", (sub, 8 - s_ if d == 0 else s_), b.w.at[wrows(X_, zsrc(d, s_), 1 - c), :])

    def multiply(X_, s_):
        j = X_ * 4 + pair(s_ - 1)

        @pl.loop(0, 5)
        def _(n):
            cs = pl.ds(pl.multiple_of(n * 256, 256), 256)
            ks = pl.ds(pl.multiple_of(j * DT, 64), DT)
            b.acc[:, cs] += jnp.dot(b.xn[j], b.w[ks, cs], preferred_element_type=F32)

    def tokx_done():
        for k, sx in enumerate((xm, xp, xo)):
            got("tokx", (k,), b.xg.at[lax.rem(sx, 2) * 4 + y, pl.ds(pl.multiple_of((sx // 2) * TB, 128), TB), :])
        for k in (0, 1):
            blk = b.xg.at[k * 4 + y]
            send("toky", (0, k, 0), blk, blk, dyp)
            send("toky", (1, k, 0), blk, blk, dym)

    def toky_first():
        for d, sy, to in ((0, ym, dyp), (1, yp, dym)):
            for k in (0, 1):
                got("toky", (d, k, 0), b.xg.at[k * 4 + sy])
            blk = b.xg.at[d * 4 + sy]
            send("toky", (d, d, 1), blk, blk, to)

    def toky_last():
        for d in (0, 1):
            got("toky", (d, d, 1), b.xg.at[d * 4 + lax.rem(y + 2, 4)])

    def norm():
        @pl.loop(0, 8)
        def _(t):
            rows = pl.ds(pl.multiple_of(t * 32, 32), 32)
            total = jnp.zeros((32, 1), F32)
            for j in range(8):
                v = b.xg[j, rows, :].astype(F32)
                total += jnp.sum(v * v, axis=1, keepdims=True)
            inv = lax.rsqrt(total / D + EPS)
            for j in range(8):
                v = b.xg[j, rows, :].astype(F32)
                b.xn[j, rows, :] = (v * inv * b.g8[j : j + 1, :]).astype(BF16)

    b.acc[...] = jnp.zeros_like(b.acc)
    ring_half(0, X, 1, 0)
    tokx_done()
    ring_half(0, X, 1, 1)
    for s_ in (2, 3):
        ring_half(0, X, s_, 0)
        ring_half(0, X, s_, 1)
    got("w1", (0,), b.w.at[wrows(1 - X, z), :])
    ring_start(1, 1 - X)
    toky_first()
    m_send()
    ring_half(0, X, 4, 0)
    ring_half(0, X, 4, 1)
    ring_half(1, 1 - X, 1, 0)
    ring_half(1, 1 - X, 1, 1)
    toky_last()
    norm()
    ready = {
        (2, 0): [(0, X, 1), (0, X, 2)],
        (2, 1): [(0, X, 3), (0, X, 4)],
        (3, 0): [(1, 1 - X, 1)],
        (3, 1): [(1, 1 - X, 2)],
    }
    for at, done in ready.items():
        ring_half(1, 1 - X, *at)
        for d in done:
            other_core(*d)
            multiply(*d[1:])
    ring_half(1, 1 - X, 4, 0)
    ring_half(1, 1 - X, 4, 1)
    for s_ in (3, 4):
        other_core(1, 1 - X, s_)
        multiply(1 - X, s_)

    @pl.loop(0, 5)
    def _(n):
        cs = pl.ds(pl.multiple_of(n * 128, 128), 128)
        g = b.acc[:, cs]
        u = b.acc[:, pl.ds(pl.multiple_of(FH + n * 128, 128), 128)]
        hid = (g / (1.0 + jnp.exp(-g)) * u).T.astype(BF16)
        for k in (0, 1):
            b.hs[k, cs, :] = hid[:, k * TB : (k + 1) * TB]

            @pl.when(c == X)
            def _():
                b.h[c * 16 + k * 8 + z, cs, :] = hid[:, k * TB : (k + 1) * TB]

    @pl.when(c != X)
    def _():
        for k in (0, 1):
            send("hx", (k,), b.hs.at[k], b.h.at[(1 - c) * 16 + k * 8 + z], dev(x_=xo, c_=1 - c))

    got("m1", (0,), b.mx.at[1 - X])
    for k in (0, 1):

        @pl.when(c != X)
        def _():
            got("hx", (k,), hchunk(k, z))

        for d in (0, 1):
            send("hr", (d, 0, k), hchunk(k, z), hchunk(k, z), dz[d])
        send("hd", (0, k), hchunk(k, z), hchunk(k, z), dc)

    def hother(k, z_):
        return b.h.at[(1 - c) * 16 + k * 8 + z_]

    def h_take(n):
        s_ = n // 2 + 1
        for k in (0, 1):

            @pl.when(lax.rem(n, 2) == k)
            def _():
                for d in (0, 1):
                    zz = lax.rem(z + (8 - s_ if d == 0 else s_), 8)
                    r = 8 - s_ if d == 0 else s_
                    ch = hchunk(k, zz)

                    def take():
                        got("hr", (d, s_ - 1, k), ch)

                        @pl.when(s_ < (4 if k == d else 3))
                        def _():
                            send("hr", (d, s_, k), ch, ch, dz[d])

                        send("hd", (r, k), ch, ch, dc)

                    if k == d:
                        take()
                    else:
                        pl.when(s_ < 4)(take)

    def level(i):
        k = (i + 1) // 2
        r = lax.rem(i + par, 2) * (8 - 2 * k) + k
        return lax.rem(r, 8), lax.rem(z + r, 8)

    def place(i):
        _, zz = level(i)
        return zz, lax.rem(zz, 2), lax.rem(zz // 2 - y + 4, 4)

    def plus(u, v):
        return (u.astype(F32) + v.astype(F32)).astype(BF16)

    xn_ = (x // 2) * 2 + 1 - xl
    dxn = dev(x_=xn_)

    def part1(units):
        at = []
        for i, k in units:
            zz, e, rel = place(i)
            r, _ = level(i)
            got("hd", (r, k), hother(k, zz))
            at.append((k * 8 + zz, e, rel))
        halves = [jnp.concatenate([b.h[f * 16 + at[0][0]], b.h[f * 16 + at[1][0]]], axis=1) for f in (0, 1)]
        for Xd in (0, 1):
            t = jnp.dot(b.mx[Xd, :, :FH], halves[0], preferred_element_type=F32)
            t += jnp.dot(b.mx[Xd, :, FH:], halves[1], preferred_element_type=F32)
            for j, (i, k) in enumerate(units):
                u = t[:, j * TB : (j + 1) * TB]
                b.q[i, k, Xd] = u[:NY].astype(BF16)

                @pl.when(xl == k)
                def _():
                    b.sx[i, Xd] = u[NY:]

                @pl.when(xl != k)
                def _():
                    b.px[i, Xd] = u[NY:].astype(BF16)

        for (i, k), (_, e, rel) in zip(units, at):

            @pl.when(xl != k)
            def _():
                send("px", (i,), b.px.at[i], b.rx.at[i], dxn)

            @pl.when(rel == 2)
            def _():
                send("qa", (e, k), b.q.at[i, k], (b.qa if k == 0 else b.qb).at[e], dyp if k == 0 else dym)

            if k == 1:

                @pl.when(rel == 1)
                def _():
                    send("qr", (e, 0), b.q.at[i, 1], b.qr.at[e, 1], dyp)

            else:

                @pl.when(rel == 3)
                def _():
                    send("qr", (e, 1), b.q.at[i, 0], b.ql.at[e, 0], dym)

    def part2s(i):
        _, e, rel = place(i)
        got("px", (i,), b.rx.at[i])
        for Xd in (0, 1):
            b.s[i, Xd] = (b.sx[i, Xd] + b.rx[i, Xd].astype(F32)).astype(BF16)

        @pl.when(rel == 2)
        def _():
            send("ya", (e, 0), b.s.at[i, 0], b.ya.at[e], dyp)
            send("ya", (e, 1), b.s.at[i, 1], b.yb.at[e], dym)

        @pl.when(rel == 1)
        def _():
            send("yr", (e, 0), b.s.at[i, 1], b.yr.at[e, 1], dyp)

        @pl.when(rel == 3)
        def _():
            send("yr", (e, 1), b.s.at[i, 0], b.yl.at[e, 0], dym)

    def part2q(i):
        _, e, rel = place(i)

        @pl.when(rel == 1)
        def _():
            got("qa", (e, 0), b.qa.at[e])
            for Xd in (0, 1):
                b.q[i, 0, Xd] = plus(b.q[i, 0, Xd], b.qa[e, Xd])
            send("qr", (e, 0), b.q.at[i, 0], b.qr.at[e, 0], dyp)

        @pl.when(rel == 3)
        def _():
            got("qa", (e, 1), b.qb.at[e])
            for Xd in (0, 1):
                b.q[i, 1, Xd] = plus(b.q[i, 1, Xd], b.qb[e, Xd])
            send("qr", (e, 1), b.q.at[i, 1], b.ql.at[e, 1], dym)

    def part3s(i):
        _, e, rel = place(i)

        @pl.when(rel == 1)
        def _():
            got("ya", (e, 0), b.ya.at[e])
            b.s[i, 0] = plus(b.s[i, 0], b.ya[e])
            send("yr", (e, 0), b.s.at[i, 0], b.yr.at[e, 0], dyp)

        @pl.when(rel == 3)
        def _():
            got("ya", (e, 1), b.yb.at[e])
            b.s[i, 1] = plus(b.s[i, 1], b.yb[e])
            send("yr", (e, 1), b.s.at[i, 1], b.yl.at[e, 1], dym)

    def part4q(i):
        _, e, rel = place(i)

        @pl.when(rel == 0)
        def _():
            got("qr", (e, 0), b.qr.at[e])
            got("qr", (e, 1), b.ql.at[e])

            @pl.loop(0, 4)
            def _(dx):
                at = (lax.rem(dx, 2), dx // 2)
                u = b.q[i, *at].astype(F32) + b.qr[e, *at].astype(F32) + b.ql[e, *at].astype(F32)
                b.tq[e, *at] = u.astype(BF16)

            for to, tx_ in ((dxo, xo), (dxp, xp), (dxm, xm)):
                send("fq", (e,), b.tq.at[e, lax.rem(tx_, 2), tx_ // 2], b.fq.at[x, e], to)
            b.fq[x, e] = b.tq[e, xl, X]

    def part4s(i):
        _, e, rel = place(i)

        @pl.when(rel == 0)
        def _():
            got("yr", (e, 0), b.yr.at[e])
            got("yr", (e, 1), b.yl.at[e])
            for Xd in (0, 1):
                b.us[e, Xd] = (
                    b.s[i, Xd].astype(F32) + b.yr[e, Xd].astype(F32) + b.yl[e, Xd].astype(F32)
                ).astype(BF16)
            send("fs", (e,), b.us.at[e, 1 - X], b.fs.at[X, e], dxo)
            b.fs[X, e] = b.us[e, X]

    def run(part, i, lag):
        pl.when((i >= lag) & (i < 8 + lag))(lambda: part(i - lag))

    part1(((0, 0), (0, 1)))

    @pl.loop(0, 13)
    def _(n):
        @pl.when(n < 8)
        def _():
            h_take(n)

        run(part2s, n, 1)
        run(part2q, n, 2)
        for k in (0, 1):

            @pl.when((lax.rem(n, 2) == k) & (n < 6))
            def _():
                part1(((n - k + 1, k), (n - k + 2, k)))

        @pl.when(n == 7)
        def _():
            part1(((7, 0), (7, 1)))

        run(part3s, n, 3)
        run(part4q, n, 5)
        run(part4s, n, 5)

    out_copy = pltpu.make_async_copy(b.ov, out, loc.at[0])

    def ph_last():
        for e in (0, 1):
            got("fq", (e,), b.fq.at[pl.ds(0, 3), e])
            got("fs", (e,), b.fs.at[0, e])
            for g in (0, 1):
                lanes = pl.ds(e * 256 + g * TB, TB)
                t = b.fq[2 * g, e].astype(F32) + b.fq[2 * g + 1, e].astype(F32)
                u = b.fs[g, e].astype(F32)
                primal = t[:KD]
                b.ov[:, lanes] = primal.astype(BF16)
                sq = 1.0 / (1.0 + jnp.exp(-primal))
                both = t[KD:] * t[KD:] + u * u
                b.cvs[:, lanes] = jnp.sum(sq * (1.0 - sq) * both, axis=0, keepdims=True)

    ph_last()

    for r in range(1, 32):
        send("cv", (0,), b.cvs, b.cvr.at[r], peers[r - 1])
    out_copy.start()
    got("cv", (0,), b.cvr.at[pl.ds(1, 31)])
    total = b.cvs[...]
    for r in range(1, 32):
        total += b.cvr[r]
    b.cvo[...] = total / (PROBES * D)
    curv_copy = pltpu.make_async_copy(b.cvo, curv, loc.at[1])
    curv_copy.start()

    def ph_drain():
        for k in range(3):
            sent("tokx", tx, k)
        sent("toky", b.xg.at[pl.ds(0, 6)])
        sent("w1", b.w.at[pl.ds(0, KD), :])
        sent("m1", b.mx.at[0])
        sent("wr", b.w.at[pl.ds(0, 14 * KD), :])
        sent("wd", b.w.at[pl.ds(0, 16 * KD), :])

        @pl.when(c != X)
        def _():
            sent("hx", b.h.at[pl.ds(0, 2)])

        sent("hr", b.h.at[pl.ds(0, 14)])
        sent("hd", b.h.at[pl.ds(0, 16)])
        sent("px", b.rx)
        sent("qa", b.q.at[pl.ds(0, 2)])
        sent("qr", b.q.at[pl.ds(0, 4)])
        sent("ya", b.rx.at[pl.ds(0, 2)])
        sent("yr", b.rx.at[pl.ds(0, 4)])
        sent("fq", b.q.at[pl.ds(0, 3), 0])
        sent("fs", b.rx.at[0])
        sent("cv", b.cvr.at[pl.ds(1, 31)])
        out_copy.wait()
        curv_copy.wait()

    ph_drain()


def on_device(tokens, norm_gain, gate_weight, up_weight, down_weight, probes):
    vmem = pl.BlockSpec(memory_space=pltpu.VMEM)
    sems = []
    for name, shape in SEMS.items():
        sems += [pltpu.SemaphoreType.DMA((3,) if name == "tokx" else (1,)), pltpu.SemaphoreType.DMA(shape)]
    out, curv = pl.pallas_call(
        kernel,
        out_shape=(jax.ShapeDtypeStruct((KD, 512), BF16), jax.ShapeDtypeStruct((1, 512), F32)),
        in_specs=[vmem] * 6,
        out_specs=(pl.BlockSpec(memory_space=pl.ANY),) * 2,
        scratch_shapes=[pltpu.VMEM(s, t) for s, t in SCRATCH.values()] + sems + [pltpu.SemaphoreType.DMA((5,))],
        compiler_params=pltpu.CompilerParams(
            collective_id=0, has_side_effects=True, vmem_limit_bytes=60 * 1024 * 1024
        ),
        name="mlp_curv",
    )(tokens.T, norm_gain.reshape(28, 128), gate_weight, up_weight, down_weight, probes)
    return out.T, curv.reshape(512)


def solution(mesh):
    return jax.shard_map(
        on_device,
        mesh=mesh,
        in_specs=(
            P("fsdp", "tp"),
            P(),
            P("fsdp", "tp"),
            P("fsdp", "tp"),
            P("fsdp", "tp"),
            P(None, "fsdp", "tp"),
        ),
        out_specs=(P("tp", "fsdp"), P("tp")),
        check_vma=False,
    )
```

time: 140 us -> 128 us (0.914)
  Pallas kernels: 137 us -> 125 us
    pallas_call x1, Pallas kernels: 137 us -> 125 us  [on_device(): pl.pallas_call(kernel, out_shape=(jax.ShapeDtypeStruct((KD, 512), BF16),...]
where the time goes in v3:
time: 128 us
  Pallas kernels  125 us (98%)
  local copies, waits for them, and re-layouts  2.14 us (2%)
    pallas_call x1, Pallas kernels, on_device(): pl.pallas_call(kernel, out_shape=(jax.ShapeDtypeStruct((KD, 512), BF16),...  125 us

profile of v3, /device:TPU:1, one launch (start us, length us, event | category | flops | bytes accessed | tf_op | source)
XLA Modules:
  0.0 128.1 jit_solution(14035018478658219716)
XLA Ops:
  0.6 125.3 %mlp_curv.1 = (bf16[112,512]{1,0:T(8,128)(2,1)}, f32[1,512]{1,0:T(1,128)}) custom-call(bf16[448,128]{1,0:T(8,128)(2,1)} %bitcast.4, bf16[28,128]{1,0:T(8,128)(2,1)} %bitcast.6, bf16[112,1280]{1,0:T(8,128)(2,1)} %wg.1, bf16[112,1280]{1,0:T(8,128)(2,1)} %wu.1, bf16[112,1280]{1,0:T(8,128)(2,1)} %dn.1, bf16[2,112,1280]{2,1,0:T(8,128)(2,1)} %pr.1), custom_call_target="tpu_custom_call" | custom-call | tf_op jit(solution)/shard_map/mlp_curv/pallas_call | solution.py:563
  126.0 0.0 copy-start
  126.0 1.6 %copy.10 = bf16[512,112]{0,1:T(8,128)(2,1)} copy(bf16[512,112]{0,1:T(8,128)(2,1)} %bitcast.5) | data formatting | bytes 229376
  127.5 0.0 copy-done
  127.5 0.6 copy.11
Async XLA Ops:
  126.0 1.6 %copy-start = (f32[1,512]{1,0:T(1,128)S(1)}, f32[1,512]{1,0:T(1,128)}, u32[]{:S(2)}) copy-start(f32[1,512]{1,0:T(1,128)} %get-tuple-element.5) | copy-start | bytes 6148

commit v4 on v3

--- a/solution.py
+++ b/solution.py
@@ -14,9 +14,12 @@
 FH = 640
 TB = 128
 DT = 448
-NY, NX = 2 * KD, KD
+NY = 176
+NX = 3 * KD - NY
 
 SCRATCH = dict(
+    tv=((DT, TB), BF16),
+    gv=((28, 128), BF16),
     xg=((8, 256, DT), BF16),
     xn=((8, 256, DT), BF16),
     g8=((8, DT), F32),
@@ -42,8 +45,6 @@
     ql=((2, 2, 2, NY, TB), BF16),
     tq=((2, 2, 2, NY, TB), BF16),
     fq=((4, 2, NY, TB), BF16),
-    ov=((KD, 512), BF16),
-    cvo=((1, 512), F32),
     cvs=((1, 512), F32),
     cvr=((32, 1, 512), F32),
 )
@@ -116,7 +117,15 @@
     def hchunk(X_, z_):
         return b.h.at[c * 16 + X_ * 8 + z_]
 
+    barrier = pltpu.get_barrier_semaphore()
+    peers = [(lax.rem(fi + r, 32), ti) for r in range(1, 32)]
+    partners = [dxp, dxm, dyp, dym] + peers
+    for p in partners:
+        pl.semaphore_signal(barrier, inc=1, device_id=p, device_id_type=MESH)
+
     mine = [
+        (tok_t, b.tv),
+        (gain, b.gv),
         (wg.at[:, cols(X)], wchunk(X, z, 0)),
         (wu.at[:, cols(X)], wchunk(X, z, 1)),
         (dn, b.mx.at[X, pl.ds(0, KD), :]),
@@ -126,55 +135,49 @@
     own = [pltpu.make_async_copy(s_, d_, loc.at[i]) for i, (s_, d_) in enumerate(mine)]
     for o in own:
         o.start()
-
+    pl.semaphore_wait(barrier, len(partners))
+    for o in own[2:4]:
+        o.wait()
+
+    def ring_start(sub, X_):
+        for h in (0, 1):
+            for d in (0, 1):
+                ch = wchunk(X_, z, h ^ d)
+                send("wr", (d, sub, 0, h ^ d), ch, ch, dz[d])
+        send("wd", (sub, 0), b.w.at[wrows(X_, z), :], b.w.at[wrows(X_, z), :], dc)
+
+    ring_start(0, X)
     tx = b.xg.at[ti, pl.ds(pl.multiple_of(X * TB, 128), TB), :]
-    tx[...] = tok_t[...].T
+    own[0].wait()
+    tx[...] = b.tv[...].T
+    for k, to in enumerate((dxp, dxm, dxo)):
+        send("tokx", (k,), tx, tx, to)
+    for half, src in enumerate((wg, wu)):
+        send("w1", (0,), src.at[:, cols(1 - X)], wchunk(X, z, half), dxo)
+    own[1].wait()
     for j in range(8):
         at = j * DT
         while at < (j + 1) * DT:
             n = min(128 - at % 128, (j + 1) * DT - at)
             row, lane = at // 128, at % 128
-            b.g8[j : j + 1, at - j * DT : at - j * DT + n] = gain[row : row + 1, lane : lane + n].astype(F32)
+            b.g8[j : j + 1, at - j * DT : at - j * DT + n] = b.gv[row : row + 1, lane : lane + n].astype(F32)
             at += n
-
-    barrier = pltpu.get_barrier_semaphore()
-    peers = [(lax.rem(fi + r, 32), ti) for r in range(1, 32)]
-    partners = [dxp, dxm, dyp, dym] + peers
-    for p in partners:
-        pl.semaphore_signal(barrier, inc=1, device_id=p, device_id_type=MESH)
-    pl.semaphore_wait(barrier, len(partners))
-
-    for o in own:
+    for o in own[4:]:
         o.wait()
 
-    def ring_start(sub, X_):
-        for half in (0, 1):
-            for d in (0, 1):
-                send("wr", (d, sub, 0, half), wchunk(X_, z, half), wchunk(X_, z, half), dz[d])
-        send("wd", (sub, 0), b.w.at[wrows(X_, z), :], b.w.at[wrows(X_, z), :], dc)
-
-    ring_start(0, X)
-    for k, to in enumerate((dxp, dxm, dxo)):
-        send("tokx", (k,), tx, tx, to)
-    for half, src in enumerate((wg, wu)):
-        send("w1", (0,), src.at[:, cols(1 - X)], wchunk(X, z, half), dxo)
-
     def m_send():
-        for k, src in enumerate((dn, pr.at[0], pr.at[1])):
-            send("m1", (0,), src, b.mx.at[X, pl.ds(k * KD, KD), :], dxo)
+        send("m1", (0,), b.mx.at[X], b.mx.at[X], dxo)
 
     def zsrc(d, s_):
         return lax.rem(z + (8 - s_ if d == 0 else s_), 8)
 
-    def ring_half(sub, X_, s_, half):
+    def ring_half(sub, X_, s_, h):
         for d in (0, 1):
-            if s_ == 4 and half != d:
-                continue
-            ch = wchunk(X_, zsrc(d, s_), half)
-            got("wr", (d, sub, s_ - 1, half), ch)
-            if s_ < 3 or (s_ == 3 and half == d):
-                send("wr", (d, sub, s_, half), ch, ch, dz[d])
-        if half == 1:
+            ch = wchunk(X_, zsrc(d, s_), h ^ d)
+            got("wr", (d, sub, s_ - 1, h ^ d), ch)
+            if s_ < 3 or (s_ == 3 and h == 0):
+                send("wr", (d, sub, s_, h ^ d), ch, ch, dz[d])
+        if h == 1 or s_ == 4:
             for d in (0, 1):
                 if s_ == 4 and d == 1:
                     continue
@@ -240,15 +243,15 @@
     ring_half(0, X, 1, 0)
     tokx_done()
     ring_half(0, X, 1, 1)
-    for s_ in (2, 3):
-        ring_half(0, X, s_, 0)
-        ring_half(0, X, s_, 1)
+    ring_half(0, X, 2, 0)
+    ring_half(0, X, 2, 1)
+    ring_half(0, X, 3, 0)
     got("w1", (0,), b.w.at[wrows(1 - X, z), :])
     ring_start(1, 1 - X)
+    ring_half(0, X, 3, 1)
     toky_first()
     m_send()
     ring_half(0, X, 4, 0)
-    ring_half(0, X, 4, 1)
     ring_half(1, 1 - X, 1, 0)
     ring_half(1, 1 - X, 1, 1)
     toky_last()
@@ -265,7 +268,6 @@
             other_core(*d)
             multiply(*d[1:])
     ring_half(1, 1 - X, 4, 0)
-    ring_half(1, 1 - X, 4, 1)
     for s_ in (3, 4):
         other_core(1, 1 - X, s_)
         multiply(1 - X, s_)
@@ -289,14 +291,14 @@
             send("hx", (k,), b.hs.at[k], b.h.at[(1 - c) * 16 + k * 8 + z], dev(x_=xo, c_=1 - c))
 
     got("m1", (0,), b.mx.at[1 - X])
-    for k in (0, 1):
+    for k, ways in ((0, ((0, 0),)), (1, ((1, 1), (0, 1), (1, 0)))):
 
         @pl.when(c != X)
         def _():
             got("hx", (k,), hchunk(k, z))
 
-        for d in (0, 1):
-            send("hr", (d, 0, k), hchunk(k, z), hchunk(k, z), dz[d])
+        for d, kk in ways:
+            send("hr", (d, 0, kk), hchunk(kk, z), hchunk(kk, z), dz[d])
         send("hd", (0, k), hchunk(k, z), hchunk(k, z), dc)
 
     def hother(k, z_):
@@ -304,28 +306,20 @@
 
     def h_take(n):
         s_ = n // 2 + 1
-        for k in (0, 1):
-
-            @pl.when(lax.rem(n, 2) == k)
+        for h in (0, 1):
+
+            @pl.when(lax.rem(n, 2) == h)
             def _():
                 for d in (0, 1):
-                    zz = lax.rem(z + (8 - s_ if d == 0 else s_), 8)
-                    r = 8 - s_ if d == 0 else s_
-                    ch = hchunk(k, zz)
-
-                    def take():
-                        got("hr", (d, s_ - 1, k), ch)
-
-                        @pl.when(s_ < (4 if k == d else 3))
-                        def _():
-                            send("hr", (d, s_, k), ch, ch, dz[d])
-
-                        send("hd", (r, k), ch, ch, dc)
-
-                    if k == d:
-                        take()
-                    else:
-                        pl.when(s_ < 4)(take)
+                    k = h ^ d
+                    ch = hchunk(k, lax.rem(z + (8 - s_ if d == 0 else s_), 8))
+                    got("hr", (d, s_ - 1, k), ch)
+
+                    @pl.when(s_ < 4 - h)
+                    def _():
+                        send("hr", (d, s_, k), ch, ch, dz[d])
+
+                    send("hd", (8 - s_ if d == 0 else s_, k), ch, ch, dc)
 
     def level(i):
         k = (i + 1) // 2
@@ -473,31 +467,35 @@
     def run(part, i, lag):
         pl.when((i >= lag) & (i < 8 + lag))(lambda: part(i - lag))
 
+    ahead = 1 - lax.rem(c + X, 2)
+    h_take(0)
+    pl.when(ahead == 1)(lambda: h_take(1))
     part1(((0, 0), (0, 1)))
-
-    @pl.loop(0, 13)
+    pl.when(ahead == 0)(lambda: h_take(1))
+
+    @pl.loop(0, 14)
     def _(n):
-        @pl.when(n < 8)
-        def _():
-            h_take(n)
-
-        run(part2s, n, 1)
+        nn = n + 2 * ahead
+
+        @pl.when((nn >= 2) & (nn < 7))
+        def _():
+            h_take(nn)
+
+        run(part2s, n, 2)
         run(part2q, n, 2)
-        for k in (0, 1):
-
-            @pl.when((lax.rem(n, 2) == k) & (n < 6))
+        for h in (0, 1):
+
+            @pl.when((lax.rem(n, 2) == h) & (n < 6))
             def _():
-                part1(((n - k + 1, k), (n - k + 2, k)))
-
-        @pl.when(n == 7)
+                part1(((n - h + 1 + par, h), (n - h + 2 - par, 1 - h)))
+
+        @pl.when(n == 6)
         def _():
             part1(((7, 0), (7, 1)))
 
-        run(part3s, n, 3)
-        run(part4q, n, 5)
-        run(part4s, n, 5)
-
-    out_copy = pltpu.make_async_copy(b.ov, out, loc.at[0])
+        run(part3s, n, 5)
+        run(part4q, n, 6)
+        run(part4s, n, 6)
 
     def ph_last():
         for e in (0, 1):
@@ -508,23 +506,24 @@
                 t = b.fq[2 * g, e].astype(F32) + b.fq[2 * g + 1, e].astype(F32)
                 u = b.fs[g, e].astype(F32)
                 primal = t[:KD]
-                b.ov[:, lanes] = primal.astype(BF16)
+                out[:, lanes] = primal.astype(BF16)
                 sq = 1.0 / (1.0 + jnp.exp(-primal))
-                both = t[KD:] * t[KD:] + u * u
-                b.cvs[:, lanes] = jnp.sum(sq * (1.0 - sq) * both, axis=0, keepdims=True)
+                slope = sq * (1.0 - sq)
+                first, rest = NY - KD, 2 * KD - NY
+                total = jnp.sum(slope[:first] * t[KD:] * t[KD:], axis=0, keepdims=True)
+                total += jnp.sum(slope[first:] * u[:rest] * u[:rest], axis=0, keepdims=True)
+                total += jnp.sum(slope * u[rest:] * u[rest:], axis=0, keepdims=True)
+                b.cvs[:, lanes] = total
 
     ph_last()
 
     for r in range(1, 32):
         send("cv", (0,), b.cvs, b.cvr.at[r], peers[r - 1])
-    out_copy.start()
     got("cv", (0,), b.cvr.at[pl.ds(1, 31)])
     total = b.cvs[...]
     for r in range(1, 32):
         total += b.cvr[r]
-    b.cvo[...] = total / (PROBES * D)
-    curv_copy = pltpu.make_async_copy(b.cvo, curv, loc.at[1])
-    curv_copy.start()
+    curv[...] = total / (PROBES * D)
 
     def ph_drain():
         for k in range(3):
@@ -549,23 +548,22 @@
         sent("fq", b.q.at[pl.ds(0, 3), 0])
         sent("fs", b.rx.at[0])
         sent("cv", b.cvr.at[pl.ds(1, 31)])
-        out_copy.wait()
-        curv_copy.wait()
 
     ph_drain()
 
 
 def on_device(tokens, norm_gain, gate_weight, up_weight, down_weight, probes):
     vmem = pl.BlockSpec(memory_space=pltpu.VMEM)
+    hbm = pl.BlockSpec(memory_space=pl.ANY)
     sems = []
     for name, shape in SEMS.items():
         sems += [pltpu.SemaphoreType.DMA((3,) if name == "tokx" else (1,)), pltpu.SemaphoreType.DMA(shape)]
     out, curv = pl.pallas_call(
         kernel,
-        out_shape=(jax.ShapeDtypeStruct((KD, 512), BF16), jax.ShapeDtypeStruct((1, 512), F32)),
-        in_specs=[vmem] * 6,
-        out_specs=(pl.BlockSpec(memory_space=pl.ANY),) * 2,
-        scratch_shapes=[pltpu.VMEM(s, t) for s, t in SCRATCH.values()] + sems + [pltpu.SemaphoreType.DMA((5,))],
+        out_shape=(pltpu.VMEM((KD, 512), BF16), pltpu.VMEM((1, 512), F32)),
+        in_specs=[hbm] * 6,
+        out_specs=(vmem, vmem),
+        scratch_shapes=[pltpu.VMEM(s, t) for s, t in SCRATCH.values()] + sems + [pltpu.SemaphoreType.DMA((7,))],
         compiler_params=pltpu.CompilerParams(
             collective_id=0, has_side_effects=True, vmem_limit_bytes=60 * 1024 * 1024
         ),

time: 128 us -> 124 us (0.969)
  Pallas kernels: 125 us -> 122 us
    pallas_call x1, Pallas kernels: 125 us -> 122 us  [on_device(): pl.pallas_call(kernel, out_shape=(pltpu.VMEM((KD, 512), BF16), pltpu.VMEM...]
where the time goes in v4:
time: 124 us; the launch traced here: 123 us
  Pallas kernels  122 us (98%)
    pallas_call x1, Pallas kernels, on_device(): pl.pallas_call(kernel, out_shape=(pltpu.VMEM((KD, 512), BF16), pltpu.VMEM...  122 us

profile of v4, /device:TPU:1, one launch (start us, length us, event | category | flops | bytes accessed | tf_op | source)
XLA Modules:
  0.0 123.5 jit_solution(14447554405836819190)
XLA Ops:
  0.6 121.6 %mlp_curv.1 = (bf16[112,512]{1,0:T(8,128)(2,1)S(1)}, f32[1,512]{1,0:T(1,128)S(1)}) custom-call(bf16[448,128]{1,0:T(8,128)(2,1)} %bitcast.6, bf16[28,128]{1,0:T(8,128)(2,1)} %bitcast.7, bf16[112,1280]{1,0:T(8,128)(2,1)} %wg.1, bf16[112,1280]{1,0:T(8,128)(2,1)} %wu.1, bf16[112,1280]{1,0:T(8,128)(2,1)} %dn.1, bf16[2,112,1280]{2,1,0:T(8,128)(2,1)} %pr.1), custom_call_target="tpu_custom_call" | custom-call | tf_op jit(solution)/shard_map/mlp_curv/pallas_call | solution.py:561
  122.3 0.6 copy.10
  122.9 0.6 copy.11

commit v5 on v4

--- a/solution.py
+++ b/solution.py
@@ -14,7 +14,7 @@
 FH = 640
 TB = 128
 DT = 448
-NY = 176
+NY = 144
 NX = 3 * KD - NY
 
 SCRATCH = dict(
@@ -268,27 +268,34 @@
             other_core(*d)
             multiply(*d[1:])
     ring_half(1, 1 - X, 4, 0)
-    for s_ in (3, 4):
-        other_core(1, 1 - X, s_)
-        multiply(1 - X, s_)
-
-    @pl.loop(0, 5)
-    def _(n):
-        cs = pl.ds(pl.multiple_of(n * 128, 128), 128)
-        g = b.acc[:, cs]
-        u = b.acc[:, pl.ds(pl.multiple_of(FH + n * 128, 128), 128)]
+    other_core(1, 1 - X, 3)
+    multiply(1 - X, 3)
+    other_core(1, 1 - X, 4)
+
+    def swap(k, rows):
+        src, dst = b.hs.at[k, rows], b.h.at[(1 - c) * 16 + k * 8 + z, rows]
+        pl.when(c != X)(lambda: send("hx", (k,), src, dst, dev(x_=xo, c_=1 - c)))
+
+    j = (1 - X) * 4 + pair(3)
+    ks = pl.ds(pl.multiple_of(j * DT, 64), DT)
+    for n in range(5):
+        cs, us = pl.ds(n * 128, 128), pl.ds(FH + n * 128, 128)
+        both = jnp.concatenate([b.w[ks, cs], b.w[ks, us]], axis=1)
+        t = jnp.dot(b.xn[j], both, preferred_element_type=F32)
+        g, u = b.acc[:, cs] + t[:, :128], b.acc[:, us] + t[:, 128:]
         hid = (g / (1.0 + jnp.exp(-g)) * u).T.astype(BF16)
         for k in (0, 1):
-            b.hs[k, cs, :] = hid[:, k * TB : (k + 1) * TB]
+            part = hid[:, k * TB : (k + 1) * TB]
+            b.hs[k, cs, :] = part
 
             @pl.when(c == X)
             def _():
-                b.h[c * 16 + k * 8 + z, cs, :] = hid[:, k * TB : (k + 1) * TB]
-
-    @pl.when(c != X)
-    def _():
-        for k in (0, 1):
-            send("hx", (k,), b.hs.at[k], b.h.at[(1 - c) * 16 + k * 8 + z], dev(x_=xo, c_=1 - c))
+                b.h[c * 16 + k * 8 + z, cs, :] = part
+
+        if n:
+            swap(0, pl.ds((n - 1) * 128, 128))
+    swap(0, pl.ds(512, 128))
+    swap(1, pl.ds(0, FH))
 
     got("m1", (0,), b.mx.at[1 - X])
     for k, ways in ((0, ((0, 0),)), (1, ((1, 1), (0, 1), (1, 0)))):
@@ -473,13 +480,11 @@
     part1(((0, 0), (0, 1)))
     pl.when(ahead == 0)(lambda: h_take(1))
 
-    @pl.loop(0, 14)
+    @pl.loop(0, 16)
     def _(n):
-        nn = n + 2 * ahead
-
-        @pl.when((nn >= 2) & (nn < 7))
-        def _():
-            h_take(nn)
+        @pl.when((n >= 2) & (n < 7))
+        def _():
+            h_take(n)
 
         run(part2s, n, 2)
         run(part2q, n, 2)
@@ -493,9 +498,9 @@
         def _():
             part1(((7, 0), (7, 1)))
 
-        run(part3s, n, 5)
-        run(part4q, n, 6)
-        run(part4s, n, 6)
+        run(part4q, n, 5)
+        run(part3s, n, 4)
+        run(part4s, n, 8)
 
     def ph_last():
         for e in (0, 1):

time: 124 us -> 121 us (0.976)
  Pallas kernels: 122 us -> 119 us
    pallas_call x1, Pallas kernels: 122 us -> 119 us  [on_device(): pl.pallas_call(kernel, out_shape=(pltpu.VMEM((KD, 512), BF16), pltpu.VMEM...]
where the time goes in v5:
time: 121 us
  Pallas kernels  119 us (98%)
  local copies, waits for them, and re-layouts  1.23 us (1%)
    pallas_call x1, Pallas kernels, on_device(): pl.pallas_call(kernel, out_shape=(pltpu.VMEM((KD, 512), BF16), pltpu.VMEM...  119 us

profile of v5, /device:TPU:1, one launch (start us, length us, event | category | flops | bytes accessed | tf_op | source)
XLA Modules:
  0.0 120.6 jit_solution(7870661492709499253)
XLA Ops:
  0.6 118.8 %mlp_curv.1 = (bf16[112,512]{1,0:T(8,128)(2,1)S(1)}, f32[1,512]{1,0:T(1,128)S(1)}) custom-call(bf16[448,128]{1,0:T(8,128)(2,1)} %bitcast.6, bf16[28,128]{1,0:T(8,128)(2,1)} %bitcast.7, bf16[112,1280]{1,0:T(8,128)(2,1)} %wg.1, bf16[112,1280]{1,0:T(8,128)(2,1)} %wu.1, bf16[112,1280]{1,0:T(8,128)(2,1)} %dn.1, bf16[2,112,1280]{2,1,0:T(8,128)(2,1)} %pr.1), custom_call_target="tpu_custom_call" | custom-call | tf_op jit(solution)/shard_map/mlp_curv/pallas_call | solution.py:566
  119.4 0.6 copy.10
  120.1 0.6 copy.11

commit v6 on v5

--- a/solution.py
+++ b/solution.py
@@ -117,12 +117,6 @@
     def hchunk(X_, z_):
         return b.h.at[c * 16 + X_ * 8 + z_]
 
-    barrier = pltpu.get_barrier_semaphore()
-    peers = [(lax.rem(fi + r, 32), ti) for r in range(1, 32)]
-    partners = [dxp, dxm, dyp, dym] + peers
-    for p in partners:
-        pl.semaphore_signal(barrier, inc=1, device_id=p, device_id_type=MESH)
-
     mine = [
         (tok_t, b.tv),
         (gain, b.gv),
@@ -133,7 +127,14 @@
         (pr.at[1], b.mx.at[X, pl.ds(2 * KD, KD), :]),
     ]
     own = [pltpu.make_async_copy(s_, d_, loc.at[i]) for i, (s_, d_) in enumerate(mine)]
-    for o in own:
+    for o in own[2:4]:
+        o.start()
+    barrier = pltpu.get_barrier_semaphore()
+    peers = [(lax.rem(fi + r, 32), ti) for r in range(1, 32)]
+    partners = [dxp, dxm, dyp, dym] + peers
+    for p in partners:
+        pl.semaphore_signal(barrier, inc=1, device_id=p, device_id_type=MESH)
+    for o in own[:2] + own[4:]:
         o.start()
     pl.semaphore_wait(barrier, len(partners))
     for o in own[2:4]:
@@ -366,27 +367,28 @@
                 def _():
                     b.px[i, Xd] = u[NY:].astype(BF16)
 
-        for (i, k), (_, e, rel) in zip(units, at):
-
-            @pl.when(xl != k)
-            def _():
-                send("px", (i,), b.px.at[i], b.rx.at[i], dxn)
-
-            @pl.when(rel == 2)
-            def _():
-                send("qa", (e, k), b.q.at[i, k], (b.qa if k == 0 else b.qb).at[e], dyp if k == 0 else dym)
-
-            if k == 1:
-
-                @pl.when(rel == 1)
+            for (i, k), (_, e, rel) in zip(units, at):
+                blk = b.q.at[i, k, Xd]
+
+                @pl.when(xl != k)
                 def _():
-                    send("qr", (e, 0), b.q.at[i, 1], b.qr.at[e, 1], dyp)
-
-            else:
-
-                @pl.when(rel == 3)
+                    send("px", (i,), b.px.at[i, Xd], b.rx.at[i, Xd], dxn)
+
+                @pl.when(rel == 2)
                 def _():
-                    send("qr", (e, 1), b.q.at[i, 0], b.ql.at[e, 0], dym)
+                    send("qa", (e, k), blk, (b.qa if k == 0 else b.qb).at[e, Xd], dyp if k == 0 else dym)
+
+                if k == 1:
+
+                    @pl.when(rel == 1)
+                    def _():
+                        send("qr", (e, 0), blk, b.qr.at[e, 1, Xd], dyp)
+
+                else:
+
+                    @pl.when(rel == 3)
+                    def _():
+                        send("qr", (e, 1), blk, b.ql.at[e, 0, Xd], dym)
 
     def part2s(i):
         _, e, rel = place(i)
@@ -522,7 +524,7 @@
 
     ph_last()
 
-    for r in range(1, 32):
+    for r in sorted(range(1, 32), key=lambda r: -min(r // 2 % 8, 8 - r // 2 % 8)):
         send("cv", (0,), b.cvs, b.cvr.at[r], peers[r - 1])
     got("cv", (0,), b.cvr.at[pl.ds(1, 31)])
     total = b.cvs[...]

time: 121 us -> 121 us (level)
  no operation moved by 1% of the time
where the time goes in v6:
time: 121 us
  Pallas kernels  119 us (98%)
  local copies, waits for them, and re-layouts  1.23 us (1%)
    pallas_call x1, Pallas kernels, on_device(): pl.pallas_call(kernel, out_shape=(pltpu.VMEM((KD, 512), BF16), pltpu.VMEM...  119 us

profile of v6, /device:TPU:1, one launch (start us, length us, event | category | flops | bytes accessed | tf_op | source)
XLA Modules:
  0.0 120.6 jit_solution(11716956667711474814)
XLA Ops:
  0.6 118.7 %mlp_curv.1 = (bf16[112,512]{1,0:T(8,128)(2,1)S(1)}, f32[1,512]{1,0:T(1,128)S(1)}) custom-call(bf16[448,128]{1,0:T(8,128)(2,1)} %bitcast.6, bf16[28,128]{1,0:T(8,128)(2,1)} %bitcast.7, bf16[112,1280]{1,0:T(8,128)(2,1)} %wg.1, bf16[112,1280]{1,0:T(8,128)(2,1)} %wu.1, bf16[112,1280]{1,0:T(8,128)(2,1)} %dn.1, bf16[2,112,1280]{2,1,0:T(8,128)(2,1)} %pr.1), custom_call_target="tpu_custom_call" | custom-call | tf_op jit(solution)/shard_map/mlp_curv/pallas_call | solution.py:568
  119.3 0.6 copy.10
  120.0 0.6 copy.11

commit v7 on v6

--- a/solution.py
+++ b/solution.py
@@ -14,7 +14,7 @@
 FH = 640
 TB = 128
 DT = 448
-NY = 144
+NY = 176
 NX = 3 * KD - NY
 
 SCRATCH = dict(

time: 121 us -> 121 us (level)
  no operation moved by 1% of the time
where the time goes in v7:
time: 121 us; the launch traced here: 120 us
  Pallas kernels  119 us (98%)
  local copies, waits for them, and re-layouts  1.23 us (1%)
    pallas_call x1, Pallas kernels, on_device(): pl.pallas_call(kernel, out_shape=(pltpu.VMEM((KD, 512), BF16), pltpu.VMEM...  119 us

profile of v7, /device:TPU:1, one launch (start us, length us, event | category | flops | bytes accessed | tf_op | source)
XLA Modules:
  0.0 120.5 jit_solution(15477679800321685535)
XLA Ops:
  0.6 118.6 %mlp_curv.1 = (bf16[112,512]{1,0:T(8,128)(2,1)S(1)}, f32[1,512]{1,0:T(1,128)S(1)}) custom-call(bf16[448,128]{1,0:T(8,128)(2,1)} %bitcast.6, bf16[28,128]{1,0:T(8,128)(2,1)} %bitcast.7, bf16[112,1280]{1,0:T(8,128)(2,1)} %wg.1, bf16[112,1280]{1,0:T(8,128)(2,1)} %wu.1, bf16[112,1280]{1,0:T(8,128)(2,1)} %dn.1, bf16[2,112,1280]{2,1,0:T(8,128)(2,1)} %pr.1), custom_call_target="tpu_custom_call" | custom-call | tf_op jit(solution)/shard_map/mlp_curv/pallas_call | solution.py:568
  119.3 0.6 copy.10
  119.9 0.6 copy.11
